TPU v7x, 128 devices: a whole 4x4x4 slice. The times are simulated.
128 devices in a mesh: tm: 32 (over y, x, core), grp: 4 (over z).
Axes of the slice: x: 4, y: 4, z: 4, core: 2. Of those that a mesh axis runs over, the one named last changes fastest.
Arguments:
- series: float32 [524288, 512], P(('tm', 'grp')), may hold values from -6 to 6
- filter_taps: float32 [33], replicated, may hold values from -1 to 1
- sign_flips: int32 [524288], P(('tm', 'grp')), may hold values from -1 to 1, as said below
- samples: int32 [8192], replicated, may hold values from 0 to 524287, as said below
Outputs:
- sketch: float32 [8192, 512], P(('tm', 'grp'))
- r_factor: float32 [512, 512], replicated
Inputs may be any that keep to these rules, and one draw needn't show every extreme that they name: `sign_flips`: each entry is -1 or +1. All distinct; the values of samples modulo 4096 take exactly 4096 distinct values, each by exactly 2 consecutive entries; entries are ordered by their value modulo 4096, then by value.
All inputs are finite; a program needn't handle non-finite values.
Results may differ from a plain program's by a relative error of at most 0.0003.
Values sent between devices are 32-bit elements; how exact they have to be, the bound alone decides.
No kernel may reach another device: no remote copies, remote signals or barrier semaphores. Data moves between devices by JAX's collectives and lax.ppermute only.
A program may use at most 128 MiB of HBM per device.

v0:
```python
import functools

import jax
import jax.numpy as jnp
import numpy as np
from jax import lax
from jax.experimental import pallas as pl
from jax.experimental.pallas import tpu as pltpu
from jax.sharding import PartitionSpec as P


F32 = jnp.float32
BF16 = jnp.bfloat16
ROWS_DEV = 4096
COLS = 512
HALF = 16
TAPS = 33
BLK = 256
WIN = BLK + 2 * HALF
ROW_SCALE = float(np.float32(1.0) / np.sqrt(np.float32(524288.0)))
Z0, CB, X0, Y0 = 0, 2, 3, 5
VMEM = pltpu.VMEM
WHOLE = pl.BlockSpec(memory_space=VMEM)
SMEM = pl.BlockSpec(memory_space=pltpu.SMEM)


def np_hadamard(order):
    ids = np.arange(order)
    both = ids[:, None] & ids[None, :]
    parity = np.zeros_like(both)
    for offset in range(order.bit_length()):
        parity ^= both >> offset & 1
    return 1 - 2 * parity


def to_partner(value, axis, delta):
    if axis == "z":
        return lax.ppermute(value, "grp", [(i, i ^ delta) for i in range(4)])
    step = {"c": delta, "x": delta << 1, "y": delta << 3}[axis]
    return lax.ppermute(value, "tm", [(i, i ^ step) for i in range(32)])


def prepare_kernel(ids_ref, taps_ref, flips_ref, band_ref, flip_ref):
    for r in range(0, BLK, 32):
        offset = lax.broadcasted_iota(jnp.int32, (32, WIN), 1) - (
            lax.broadcasted_iota(jnp.int32, (32, WIN), 0) + r
        )
        band = jnp.zeros((32, WIN), F32)
        for k in range(TAPS):
            band = jnp.where(offset == k, taps_ref[k], band)
        high = band.astype(BF16)
        low = (band - high.astype(F32)).astype(BF16)
        band_ref[r : r + 32, :] = jnp.concatenate([high, high, low], 1)
    times = lax.broadcasted_iota(jnp.int32, (16, 128), 0) * BLK + lax.broadcasted_iota(
        jnp.int32, (16, 128), 1
    )
    for h in range(2):
        both = (times + 128 * h) & (ids_ref[3] * 32)
        for shift in (8, 4, 2, 1):
            both = both ^ lax.shift_right_logical(both, shift)
        signs = flips_ref[pl.ds(h, 16, stride=2), :] * (1 - 2 * (both & 1))
        flip_ref[:, 128 * h : 128 * h + 128] = signs.astype(F32)


def owners_kernel(ids_ref, samples_ref, a_ref, b_ref, turn_ref):
    yx, core, z = ids_ref[0], ids_ref[1], ids_ref[2]

    def turned(block, half, slot):
        line = lax.shift_right_logical(samples_ref[pl.ds(block * 2 + half, 1), :], 12).astype(F32)
        turn_ref[slot] = jnp.broadcast_to(line, (128, 128)).T

    def column(slot, s, low):
        return turn_ref[slot, pl.ds(low * 64 + s, 32, stride=2), :].astype(jnp.int32)

    for y in range(4):
        for c in range(2):
            for x in range(4):
                turned((yx ^ (y * 4 + x)) * 2 + (core ^ c), z // 2, x)
                for s in range(2):
                    a_ref[s, y, x, c] = jnp.where(z % 2 == 1, column(x, s, 1), column(x, s, 0))
            for h in range(2):
                turned((yx ^ (y * 4)) * 2 + (core ^ c), h, 4 + h)
                for s in range(2):
                    for low in range(2):
                        b_ref[s, y, c, z ^ (2 * h + low)] = column(4 + h, s, low)


def local_kernel(by_z, x_ref, prev_ref, next_ref, band_ref, had_ref, flip_ref, *refs):
    outs, mid_ref = refs[:4], refs[4]
    for b in range(16):
        if b == 0:
            window = jnp.concatenate([prev_ref[...], x_ref[0 : BLK + HALF]], 0)
        elif b == 15:
            window = jnp.concatenate([x_ref[b * BLK - HALF :], next_ref[...]], 0)
        else:
            window = x_ref[b * BLK - HALF : (b + 1) * BLK + HALF]
        high = window.astype(BF16)
        low = (window - high.astype(F32)).astype(BF16)
        stacked = jnp.concatenate([high, low, high], 0)
        mid_ref[b] = jnp.dot(band_ref[...], stacked, preferred_element_type=F32)
    for b in range(16):
        filtered = mid_ref[b]
        f_high = filtered.astype(BF16)
        f_low = (filtered - f_high.astype(F32)).astype(BF16)
        signed = had_ref[...] * flip_ref[b : b + 1, :].astype(BF16)
        mid_ref[b] = jnp.dot(
            jnp.concatenate([signed, signed], 1),
            jnp.concatenate([f_high, f_low], 0),
            preferred_element_type=F32,
        )

    def butterflies(at):
        vals = [mid_ref[b, pl.ds(at, 8), :] for b in range(16)]
        for half in (8, 4, 2, 1):
            vals = [
                vals[i] + vals[i + half] if not i & half else vals[i - half] - vals[i]
                for i in range(16)
            ]
        return vals

    def rows_of_z(d, r, _):
        core, part = r // 4, r % 4
        vals = butterflies(pl.multiple_of(core * 128 + d * 32 + part * 8, 8))
        for i in range(16):
            outs[d][i, pl.ds(pl.multiple_of(r * 8, 8), 8), :] = vals[i]
        return 0

    def rows_all(r, _):
        at = pl.multiple_of(r * 8, 8)
        vals = butterflies(at)
        for i in range(16):
            outs[i % 4][i // 4, pl.ds(at, 8), :] = vals[i]
        return 0

    if by_z:
        for d in range(4):
            lax.fori_loop(0, 8, functools.partial(rows_of_z, d), 0)
    else:
        lax.fori_loop(0, 32, rows_all, 0)


def sign_of(owner, bit, width):
    e = (1 - 2 * (lax.shift_right_logical(owner, bit) & 1)).astype(F32)
    return jnp.concatenate([e] * (width // 128), -1) if width > 128 else e


def core_kernel(keep_ref, recv_ref, o_ref, *outs):
    for s in range(2):
        for y in range(4):
            for d in range(4):
                e = sign_of(o_ref[s, y, d], CB, 256)
                outs[y][s, d] = keep_ref[s, y, d] + e * recv_ref[s, y, d]


def core_stage(keep, recv, owners, block):
    whole = pl.BlockSpec(keep.shape, lambda i: (0,) * 5)
    return pl.pallas_call(
        core_kernel,
        grid=(1,),
        in_specs=[whole, whole, pl.BlockSpec(block, lambda i: (0,) * 6)],
        out_specs=[pl.BlockSpec((2, 4, 32, 256), lambda i: (0,) * 4)] * 4,
        out_shape=[jax.ShapeDtypeStruct((2, 4, 32, 256), F32)] * 4,
    )(keep, recv, owners)


def merged(parts, owner, bit):
    width = parts[0].shape[-1]
    e0, e1 = sign_of(owner, bit, width), sign_of(owner, bit + 1, width)
    return (parts[0] + e0 * parts[1]) + e1 * (parts[2] + e0 * parts[3])


def merge_kernel(bit, cut, *refs):
    ins, o_ref, outs = refs[:4], refs[4], refs[5:]
    lead = ins[0].shape[1:-2]
    for s in range(2):
        for at in np.ndindex(*lead):
            value = merged([r[(s, *at)] for r in ins], o_ref[(s, *at)], bit)
            rest = tuple(v for d, v in enumerate(at) if d != cut)
            outs[at[cut]][(s, *rest)] = value


def first_kernel(bit, core_dim, *refs):
    ins, o_ref, outs = refs[:4], refs[4], refs[5:]
    lead = ins[0].shape[1:-2]
    for at in np.ndindex(*lead):
        parts = [r[(0, *at)] for r in ins]
        rest = tuple(v for d, v in enumerate(at) if d != core_dim)
        for s in range(2):
            outs[at[core_dim]][(s, 0, *rest)] = merged(parts, o_ref[(s, 0, *at)], bit)


def first_stage(parts, owners, bit, core_dim):
    lead = parts[0].shape[1:-2]
    return pl.pallas_call(
        functools.partial(first_kernel, bit, core_dim),
        grid=(4,),
        in_specs=[pl.BlockSpec((1, *lead, 32, 256), lambda i: (i, 0, 0, 0, 0))] * 4
        + [pl.BlockSpec((2, 1, *lead, 32, 128), lambda i: (0, i, 0, 0, 0, 0))],
        out_specs=[pl.BlockSpec((2, 1, 4, 32, 256), lambda i: (0, i, 0, 0, 0))] * 2,
        out_shape=[jax.ShapeDtypeStruct((2, 4, 4, 32, 256), F32)] * 2,
    )(*parts, owners)


def merge_stage(parts, owners, bit, cut, block):
    shape = parts[0].shape
    out = tuple(v for d, v in enumerate(shape) if d != cut + 1)
    whole = lambda dims: pl.BlockSpec(dims, lambda i: (0,) * len(dims))
    return pl.pallas_call(
        functools.partial(merge_kernel, bit, cut),
        grid=(1,),
        in_specs=[whole(shape)] * 4 + [pl.BlockSpec(block, lambda i: (0,) * 6)],
        out_specs=[whole(out)] * 4,
        out_shape=[jax.ShapeDtypeStruct(out, F32)] * 4,
    )(*parts, owners)


def final_kernel(ids_ref, *refs):
    a_in, b_in = refs[0:4], refs[4:8]
    o_ref, sketch_ref, keep_ref, send_ref, gram_ref = refs[8:]
    core, z, me = ids_ref[1], ids_ref[2], ids_ref[3]
    halves = []
    for s in range(2):
        owner = o_ref[s]
        parity = owner & me
        parity = parity ^ lax.shift_right_logical(parity, 4)
        parity = parity ^ lax.shift_right_logical(parity, 2)
        parity = parity ^ lax.shift_right_logical(parity, 1)
        factor = (1 - 2 * (parity & 1)).astype(F32) * ROW_SCALE
        left = merged([r[s] for r in a_in], owner, X0)
        right = merged([r[s] for r in b_in], owner, Z0)
        rows = jnp.concatenate([left, right], 1) * jnp.concatenate([factor] * 4, 1)
        sketch_ref[:, s, :] = rows
        halves.append(rows)
    both = jnp.concatenate(halves, 0)
    gram_ref[...] = lax.dot_general(
        both, both, (((0,), (0,)), ((), ())),
        precision=lax.Precision.HIGHEST, preferred_element_type=F32,
    )
    for d in range(4):
        for ref, slot in ((keep_ref, core * 4 + (z ^ d)), (send_ref, (1 - core) * 4 + (z ^ d))):
            for t in range(3):
                ref[d, :, 128 * t : 128 * t + 128] = gram_ref[gram_block(slot, t)]


def gram_block(slot, t):
    row = pl.multiple_of(slot * 64, 64)
    col = pl.multiple_of(((slot // 2 + t) & 3) * 128, 128)
    return pl.ds(row, 64), pl.ds(col, 128)


def lane(tile, at):
    ids = lax.broadcasted_iota(jnp.int32, (8, 128), 1)
    return jnp.broadcast_to(jnp.sum(jnp.where(ids == at, tile, 0.0), axis=1, keepdims=True), (8, 128))


def sub(tile, at):
    return jnp.broadcast_to(tile[at : at + 1, :], tile.shape)


def wide(tile, width):
    return jnp.concatenate([tile] * (width // 128), 1) if width > 128 else tile


def cholesky_kernel(ids_ref, s0, s1, s2, s3, p_ref, out_ref, g_ref):
    core, z = ids_ref[1], ids_ref[2]
    for d, mine in enumerate((s0, s1, s2, s3)):
        for t in range(3):
            cut = slice(128 * t, 128 * t + 128)
            g_ref[gram_block(core * 4 + (z ^ d), t)] = mine[:, cut] * (1.0 / 8192)
            g_ref[gram_block((1 - core) * 4 + (z ^ d), t)] = p_ref[d, :, cut] * (1.0 / 8192)
    g_ref[0:128, 384:512] = g_ref[384:512, 0:128].T
    below = lax.broadcasted_iota(jnp.int32, (8, 128), 0)
    step = 32
    for base in range(0, COLS, step):
        lead = base // 128 * 128
        off, width = base - lead, COLS - lead
        row8 = lax.broadcasted_iota(jnp.int32, (8, width), 0)
        col8 = lax.broadcasted_iota(jnp.int32, (8, width), 1)
        tiles = [g_ref[base + 8 * p : base + 8 * p + 8, lead:] for p in range(step // 8)]
        done = []
        for p in range(step // 8):
            cols = [[lane(t[:, :128], off + 8 * p + i) for i in range(8)] for t in tiles[p:]]
            pivots = jnp.ones((8, 128), F32)
            for i in range(8):
                pivot = sub(cols[0][i], i)
                pivots = jnp.where(below == i, pivot, pivots)
                inverse = 1.0 / pivot
                line = sub(tiles[p], i)
                factors = [c[i] * inverse for c in cols]
                factors[0] = jnp.where(below > i, factors[0], 0.0)
                for k in range(i + 1, 8):
                    row = sub(cols[0][k], i)
                    for n, c in enumerate(cols):
                        c[k] = c[k] - factors[n] * row
                for n, f in enumerate(factors):
                    tiles[p + n] = tiles[p + n] - wide(f, width) * line
            rows = tiles[p] * wide(lax.rsqrt(pivots), width)
            rows = jnp.where(col8 >= row8 + (off + 8 * p), rows, 0.0)
            at = base + 8 * p
            out_ref[at : at + 8, lead:] = rows
            if lead:
                out_ref[at : at + 8, :lead] = jnp.zeros((8, lead), F32)
            done.append(rows)
        after = base + step
        if after < COLS:
            left = after // 128 * 128
            rows = jnp.concatenate(done, 0)[:, left - lead :]
            one = rows.astype(BF16)
            rest = rows - one.astype(F32)
            two = rest.astype(BF16)
            three = (rest - two.astype(F32)).astype(BF16)
            update = lax.dot_general(
                jnp.concatenate([one, one, two, one, three, two], 0),
                jnp.concatenate([one, two, one, three, one, two], 0),
                (((0,), (0,)), ((), ())), preferred_element_type=F32,
            )
            g_ref[after:, left:] -= update[after - left :, :]


def spread(parts, axis):
    moved = [parts[0]]
    for d in (1, 2, 3):
        moved.append(to_partner(parts[d], axis, d))
    return moved


def summed(value, axis):
    one, two, three = (to_partner(value, axis, d) for d in (1, 2, 3))
    return (value + one) + (two + three)


def on_device(series, filter_taps, sign_flips, samples):
    tm, z = lax.axis_index("tm"), lax.axis_index("grp")
    me = tm * 4 + z
    ids = jnp.stack([tm // 2, tm % 2, z, me]).astype(jnp.int32)

    up = [(i, i + 1) for i in range(127)]
    prev = lax.ppermute(series[ROWS_DEV - HALF :], ("tm", "grp"), up)
    nxt = lax.ppermute(series[:HALF], ("tm", "grp"), [(b, a) for a, b in up])

    had = jnp.asarray(np_hadamard(BLK), BF16)
    bands, flips = pl.pallas_call(
        prepare_kernel,
        in_specs=[SMEM, SMEM, WHOLE],
        out_specs=[WHOLE] * 2,
        out_shape=[
            jax.ShapeDtypeStruct((BLK, 3 * WIN), BF16),
            jax.ShapeDtypeStruct((16, BLK), F32),
        ],
    )(ids, filter_taps, sign_flips.reshape(32, 128))

    firsts = []
    for half in range(2):
        cut = lambda i, half=half: (0, half)
        out = (16, 64, 256) if half == 0 else (4, 256, 256)
        parts = pl.pallas_call(
            functools.partial(local_kernel, half == 0),
            grid=(1,),
            in_specs=[
                pl.BlockSpec((ROWS_DEV, 256), cut),
                pl.BlockSpec((HALF, 256), cut),
                pl.BlockSpec((HALF, 256), cut),
                pl.BlockSpec((BLK, 3 * WIN), lambda i: (0, 0)),
                pl.BlockSpec((BLK, BLK), lambda i: (0, 0)),
                pl.BlockSpec((16, BLK), lambda i: (0, 0)),
            ],
            out_specs=[pl.BlockSpec(out, lambda i: (0, 0, 0))] * 4,
            out_shape=[jax.ShapeDtypeStruct(out, F32)] * 4,
            scratch_shapes=[VMEM((16, BLK, 256), F32)],
        )(series, prev, nxt, bands, had, flips)
        shape = (4, 4, 2, 32, 256) if half == 0 else (4, 2, 4, 32, 256)
        firsts.append([p.reshape(shape) for p in parts])

    a = spread(firsts[0], "z")
    b = spread(firsts[1], "x")
    late, b[0] = lax.optimization_barrier((samples.reshape(64, 128), b[0]))
    owners_a, owners_b = pl.pallas_call(
        owners_kernel,
        in_specs=[SMEM, WHOLE],
        out_specs=[WHOLE] * 2,
        out_shape=[
            jax.ShapeDtypeStruct((2, 4, 4, 2, 32, 128), jnp.int32),
            jax.ShapeDtypeStruct((2, 4, 2, 4, 32, 128), jnp.int32),
        ],
        scratch_shapes=[VMEM((6, 128, 128), F32)],
    )(ids, late)

    none = None
    keep, send = first_stage(a, owners_a, Z0, 1)
    a = list(core_stage(keep, to_partner(send, "c", 1), owners_a, (2, 4, 4, none, 32, 128)))
    a = spread(a, "y")
    keep, send = first_stage(b, owners_b, X0, 0)
    b = core_stage(keep, to_partner(send, "c", 1), owners_b, (2, 4, none, 4, 32, 128))
    b = spread(b, "y")
    a = merge_stage(a, owners_a, Y0, 0, (2, none, 4, none, 32, 128))
    a = spread(a, "x")
    b = merge_stage(b, owners_b, Y0, 0, (2, none, none, 4, 32, 128))
    b = spread(b, "z")

    sketch, keep, send = pl.pallas_call(
        final_kernel,
        grid=(1,),
        in_specs=[SMEM] + [WHOLE] * 8
        + [pl.BlockSpec((2, none, none, none, 32, 128), lambda i: (0,) * 6)],
        out_specs=[WHOLE] * 3,
        out_shape=[
            jax.ShapeDtypeStruct((32, 2, COLS), F32),
            jax.ShapeDtypeStruct((4, 64, 384), F32),
            jax.ShapeDtypeStruct((4, 64, 384), F32),
        ],
        scratch_shapes=[VMEM((COLS, COLS), F32)],
    )(ids, *a, *b, owners_a)
    sketch = sketch.reshape(64, COLS)

    held = keep + to_partner(send, "c", 1)
    one, two, three = (to_partner(held[d], "z", d) for d in (1, 2, 3))
    share = (held[0] + one) + (two + three)
    share = summed(share, "x")
    share = summed(share, "y")
    near = [share] + [to_partner(share, "z", d) for d in (1, 2, 3)]
    far = to_partner(jnp.stack(near), "c", 1)

    r_factor = pl.pallas_call(
        cholesky_kernel,
        in_specs=[SMEM] + [WHOLE] * 5,
        out_specs=WHOLE,
        out_shape=jax.ShapeDtypeStruct((COLS, COLS), F32),
        scratch_shapes=[VMEM((COLS, COLS), F32)],
    )(ids, *near, far)
    return (sketch, r_factor)


def solution(mesh):
    return jax.shard_map(
        on_device,
        mesh=mesh,
        in_specs=(P(("tm", "grp"), None), P(), P(("tm", "grp")), P()),
        out_specs=(P(("tm", "grp"), None), P()),
        check_vma=False,
    )
```

profile of v0, /device:TPU:1, one launch (start us, length us, event | category | flops | bytes accessed | tf_op | source)
XLA Modules:
  0.0 209.9 jit_solution(17138884364075032120)
XLA Ops:
  0.6 0.8 fusion.2
  1.4 7.0 %collective-permute-start.1 = (f32[16,512]{1,0:T(8,128)S(1)}, f32[16,512]{1,0:T(8,128)S(1)}, u32[]{:S(2)}, u32[]{:S(2)}) collective-permute-start(f32[16,512]{1,0:T(8,128)S(1)} %get-tuple-element.76), channel_id=1, source_target_pairs={{1,0},{2,1},{3,2},{4,3},{5,4},{6,5},{7,6},{8,7},{9,8},{10,9},{11,1... | collective-permute-start | bytes 98312 | tf_op jit(solution)/shard_map/ppermute | solution.py:339
  8.5 1.9 collective-permute-start
  11.0 2.0 shard_map.68
  13.0 1.9 collective-permute-done.prev_ref
  14.9 0.6 copy-done.17
  15.5 8.8 %shard_map.70 = (f32[4,256,256]{2,1,0:T(8,128)}, f32[4,256,256]{2,1,0:T(8,128)}, f32[4,256,256]{2,1,0:T(8,128)}, f32[4,256,256]{2,1,0:T(8,128)}) custom-call(f32[4096,512]{1,0:T(8,128)} %x_ref.3, f32[16,512]{1,0:T(8,128)} %copy-done.17, f32[16,512]{1,0:T(8,128)} %copy-done.16, bf16[256,864]{1,0:T(8,128)(2,1)} %get-tuple-element.39.band_ref, ...), custom_call_target="tpu_custom_call" | custom-call | tf_op jit(solution)/shard_map/pallas_call | solution.py:356
  24.3 1.6 collective-permute-start.12
  25.9 2.4 %collective-permute-start.13 = (f32[4,2,4,32,256]{4,3,2,1,0:T(8,128)}, f32[4,2,4,32,256]{4,3,2,1,0:T(8,128)}, u32[]{:S(2)}, u32[]{:S(2)}) collective-permute-start(f32[4,2,4,32,256]{4,3,2,1,0:T(8,128)} %bitcast.42), channel_id=1, source_target_pairs={{0,16},{4,20},{8,24},{12,28},{16,0},{20,4},{24,8},{28,12},{32,48},... | collective-permute-start | bytes 3145736 | tf_op jit(solution)/shard_map/ppermute | solution.py:40
  28.3 9.0 %shard_map.69 = (f32[16,64,256]{2,1,0:T(8,128)}, f32[16,64,256]{2,1,0:T(8,128)}, f32[16,64,256]{2,1,0:T(8,128)}, f32[16,64,256]{2,1,0:T(8,128)}) custom-call(f32[4096,512]{1,0:T(8,128)} %x_ref.3, f32[16,512]{1,0:T(8,128)} %copy-done.17, f32[16,512]{1,0:T(8,128)} %copy-done.16, bf16[256,864]{1,0:T(8,128)(2,1)} %get-tuple-element.39.band_ref, ...), custom_call_target="tpu_custom_call" | custom-call | tf_op jit(solution)/shard_map/pallas_call | solution.py:356
  37.4 4.3 %collective-permute-start.3 = (f32[4,4,2,32,256]{4,3,2,1,0:T(8,128)}, f32[4,4,2,32,256]{4,3,2,1,0:T(8,128)S(1)}, u32[]{:S(2)}, u32[]{:S(2)}) collective-permute-start(f32[4,4,2,32,256]{4,3,2,1,0:T(8,128)} %bitcast.39), channel_id=1, source_target_pairs={{0,2},{1,3},{2,0},{3,1},{4,6},{5,7},{6,4},{7,5},{8,10},{9,11},{10,... | collective-permute-start | bytes 3145736 | tf_op jit(solution)/shard_map/ppermute | solution.py:38
  41.7 7.6 %collective-permute-done.12.refs_1_ = f32[4,2,4,32,256]{4,3,2,1,0:T(8,128)S(1)} collective-permute-done((f32[4,2,4,32,256]{4,3,2,1,0:T(8,128)}, f32[4,2,4,32,256]{4,3,2,1,0:T(8,128)S(1)}, u32[]{:S(2)}, u32[]{:S(2)}) %collective-permute-start.12) | collective-permute-done | bytes 1048608 | tf_op jit(solution)/shard_map/ppermute | solution.py:40
  49.3 1.6 collective-permute-start.4
  50.9 3.2 %shard_map.71 = (s32[2,4,4,2,32,128]{5,4,3,2,1,0:T(8,128)}, s32[2,4,2,4,32,128]{5,4,3,2,1,0:T(8,128)}) custom-call(s32[4]{0:T(128)} %pad_add_fusion.ids_ref, s32[64,128]{1,0:T(8,128)} %bitcast.36), custom_call_target="tpu_custom_call" | custom-call | tf_op jit(solution)/shard_map/pallas_call | solution.py:377
  54.2 19.5 %collective-permute-done.13.refs_2_ = f32[4,2,4,32,256]{4,3,2,1,0:T(8,128)} collective-permute-done((f32[4,2,4,32,256]{4,3,2,1,0:T(8,128)}, f32[4,2,4,32,256]{4,3,2,1,0:T(8,128)}, u32[]{:S(2)}, u32[]{:S(2)}) %collective-permute-start.13) | collective-permute-done | bytes 1048608 | tf_op jit(solution)/shard_map/ppermute | solution.py:40
  73.6 2.1 collective-permute-done.14.refs_3_
  75.7 4.6 %shard_map.75 = (f32[2,4,4,32,256]{4,3,2,1,0:T(8,128)}, f32[2,4,4,32,256]{4,3,2,1,0:T(8,128)}) custom-call(f32[4,2,4,32,256]{4,3,2,1,0:T(8,128)} %bitcast.31, f32[4,2,4,32,256]{4,3,2,1,0:T(8,128)} %copy-done.1, f32[4,2,4,32,256]{4,3,2,1,0:T(8,128)} %collective-permute-done.13.refs_2_, f32[4,2,4,32,256]{4,3,2,1,0:T(8,128)} %collective-permute-done.14.refs_3_, ...), custom_call_target="tpu_custom_call" | custom-call | tf_op jit(solution)/shard_map/pallas_call | solution.py:194
  80.4 2.2 %collective-permute-start.15 = (f32[2,4,4,32,256]{4,3,2,1,0:T(8,128)}, f32[2,4,4,32,256]{4,3,2,1,0:T(8,128)S(1)}, u32[]{:S(2)}, u32[]{:S(2)}) collective-permute-start(f32[2,4,4,32,256]{4,3,2,1,0:T(8,128)} %get-tuple-element.64), channel_id=1, source_target_pairs={{0,4},{4,0},{8,12},{12,8},{16,20},{20,16},{24,28},{28,24},{32,36},... | collective-permute-start | bytes 3145736 | tf_op jit(solution)/shard_map/ppermute | solution.py:40
  82.5 4.5 %collective-permute-done.3.refs_2_ = f32[4,4,2,32,256]{4,3,2,1,0:T(8,128)S(1)} collective-permute-done((f32[4,4,2,32,256]{4,3,2,1,0:T(8,128)}, f32[4,4,2,32,256]{4,3,2,1,0:T(8,128)S(1)}, u32[]{:S(2)}, u32[]{:S(2)}) %collective-permute-start.3) | collective-permute-done | bytes 1048608 | tf_op jit(solution)/shard_map/ppermute | solution.py:38
  87.1 9.4 %collective-permute-done.4.refs_3_ = f32[4,4,2,32,256]{4,3,2,1,0:T(8,128)} collective-permute-done((f32[4,4,2,32,256]{4,3,2,1,0:T(8,128)}, f32[4,4,2,32,256]{4,3,2,1,0:T(8,128)}, u32[]{:S(2)}, u32[]{:S(2)}) %collective-permute-start.4) | collective-permute-done | bytes 1048608 | tf_op jit(solution)/shard_map/ppermute | solution.py:38
  96.5 4.7 %shard_map.72 = (f32[2,4,4,32,256]{4,3,2,1,0:T(8,128)}, f32[2,4,4,32,256]{4,3,2,1,0:T(8,128)}) custom-call(f32[4,4,2,32,256]{4,3,2,1,0:T(8,128)} %bitcast.30, f32[4,4,2,32,256]{4,3,2,1,0:T(8,128)} %copy-done, f32[4,4,2,32,256]{4,3,2,1,0:T(8,128)} %copy-done.2, f32[4,4,2,32,256]{4,3,2,1,0:T(8,128)} %collective-permute-done.4.refs_3_, ...), custom_call_target="tpu_custom_call" | custom-call | tf_op jit(solution)/shard_map/pallas_call | solution.py:194
  101.2 2.4 %collective-permute-start.5 = (f32[2,4,4,32,256]{4,3,2,1,0:T(8,128)}, f32[2,4,4,32,256]{4,3,2,1,0:T(8,128)S(1)}, u32[]{:S(2)}, u32[]{:S(2)}) collective-permute-start(f32[2,4,4,32,256]{4,3,2,1,0:T(8,128)} %get-tuple-element.49), channel_id=1, source_target_pairs={{0,4},{4,0},{8,12},{12,8},{16,20},{20,16},{24,28},{28,24},{32,36},... | collective-permute-start | bytes 3145736 | tf_op jit(solution)/shard_map/ppermute | solution.py:40
  103.5 1.0 copy-done.3
  104.5 2.7 %shard_map.76 = (f32[2,4,32,256]{3,2,1,0:T(8,128)}, f32[2,4,32,256]{3,2,1,0:T(8,128)}, f32[2,4,32,256]{3,2,1,0:T(8,128)}, f32[2,4,32,256]{3,2,1,0:T(8,128)}) custom-call(f32[2,4,4,32,256]{4,3,2,1,0:T(8,128)} %get-tuple-element.63.keep_ref, f32[2,4,4,32,256]{4,3,2,1,0:T(8,128)} %copy-done.3, s32[2,4,2,4,32,128]{5,4,3,2,1,0:T(8,128)} %get-tuple-element.62.refs_4_.o_ref), custom_call_target="tpu_custom_call" | custom-call | tf_op jit(solution)/shard_map/pallas_call | solution.py:157
  107.5 2.6 %collective-permute-start.17 = (f32[2,4,32,256]{3,2,1,0:T(8,128)}, f32[2,4,32,256]{3,2,1,0:T(8,128)S(1)}, u32[]{:S(2)}, u32[]{:S(2)}) collective-permute-start(f32[2,4,32,256]{3,2,1,0:T(8,128)} %get-tuple-element.67), channel_id=1, source_target_pairs={{0,64},{4,68},{8,72},{12,76},{16,80},{20,84},{24,88},{28,92},{32,9... | collective-permute-start | bytes 786440 | tf_op jit(solution)/shard_map/ppermute | solution.py:40
  110.1 1.0 collective-permute-start.18
  111.1 1.0 copy-done.4
  112.1 2.7 %shard_map.73 = (f32[2,4,32,256]{3,2,1,0:T(8,128)}, f32[2,4,32,256]{3,2,1,0:T(8,128)}, f32[2,4,32,256]{3,2,1,0:T(8,128)}, f32[2,4,32,256]{3,2,1,0:T(8,128)}) custom-call(f32[2,4,4,32,256]{4,3,2,1,0:T(8,128)} %get-tuple-element.48.keep_ref, f32[2,4,4,32,256]{4,3,2,1,0:T(8,128)} %copy-done.4, s32[2,4,4,2,32,128]{5,4,3,2,1,0:T(8,128)} %get-tuple-element.47.refs_4_.o_ref.refs_8_), custom_call_target="tpu_custom_call" | custom-call | tf_op jit(solution)/shard_map/pallas_call | solution.py:157
  114.8 2.9 %collective-permute-start.7 = (f32[2,4,32,256]{3,2,1,0:T(8,128)}, f32[2,4,32,256]{3,2,1,0:T(8,128)S(1)}, u32[]{:S(2)}, u32[]{:S(2)}) collective-permute-start(f32[2,4,32,256]{3,2,1,0:T(8,128)} %get-tuple-element.52), channel_id=1, source_target_pairs={{0,64},{4,68},{8,72},{12,76},{16,80},{20,84},{24,88},{28,92},{32,9... | collective-permute-start | bytes 786440 | tf_op jit(solution)/shard_map/ppermute | solution.py:40
  117.6 1.0 collective-permute-start.8
  118.6 3.7 %collective-permute-done.17.refs_2_ = f32[2,4,32,256]{3,2,1,0:T(8,128)S(1)} collective-permute-done((f32[2,4,32,256]{3,2,1,0:T(8,128)}, f32[2,4,32,256]{3,2,1,0:T(8,128)S(1)}, u32[]{:S(2)}, u32[]{:S(2)}) %collective-permute-start.17) | collective-permute-done | bytes 262176 | tf_op jit(solution)/shard_map/ppermute | solution.py:40
  122.4 2.1 collective-permute-done.18.refs_3_
  124.4 0.7 copy-done.15
  125.2 2.0 shard_map.77
  127.2 3.9 %collective-permute-start.20 = (f32[2,32,256]{2,1,0:T(8,128)}, f32[2,32,256]{2,1,0:T(8,128)S(1)}, u32[]{:S(2)}, u32[]{:S(2)}) collective-permute-start(f32[2,32,256]{2,1,0:T(8,128)} %get-tuple-element.71), channel_id=1, source_target_pairs={{0,2},{1,3},{2,0},{3,1},{4,6},{5,7},{6,4},{7,5},{8,10},{9,11},{10,... | collective-permute-start | bytes 196616 | tf_op jit(solution)/shard_map/ppermute | solution.py:38
  131.0 2.6 %collective-permute-done.7.refs_2_ = f32[2,4,32,256]{3,2,1,0:T(8,128)S(1)} collective-permute-done((f32[2,4,32,256]{3,2,1,0:T(8,128)}, f32[2,4,32,256]{3,2,1,0:T(8,128)S(1)}, u32[]{:S(2)}, u32[]{:S(2)}) %collective-permute-start.7) | collective-permute-done | bytes 262176 | tf_op jit(solution)/shard_map/ppermute | solution.py:40
  133.6 2.0 collective-permute-done.8.refs_3_
  135.7 0.7 copy-done.13
  136.4 2.0 shard_map.74
  138.3 1.2 collective-permute-start.9
  139.5 4.1 %collective-permute-start.10 = (f32[2,32,256]{2,1,0:T(8,128)}, f32[2,32,256]{2,1,0:T(8,128)S(1)}, u32[]{:S(2)}, u32[]{:S(2)}) collective-permute-start(f32[2,32,256]{2,1,0:T(8,128)} %get-tuple-element.56), channel_id=1, source_target_pairs={{0,16},{4,20},{8,24},{12,28},{16,0},{20,4},{24,8},{28,12},{32,48},... | collective-permute-start | bytes 196616 | tf_op jit(solution)/shard_map/ppermute | solution.py:40
  143.7 2.5 %collective-permute-done.10.refs_2_ = f32[2,32,256]{2,1,0:T(8,128)S(1)} collective-permute-done((f32[2,32,256]{2,1,0:T(8,128)}, f32[2,32,256]{2,1,0:T(8,128)S(1)}, u32[]{:S(2)}, u32[]{:S(2)}) %collective-permute-start.10) | collective-permute-done | bytes 65568 | tf_op jit(solution)/shard_map/ppermute | solution.py:40
  146.2 2.3 %collective-permute-done.11.refs_3_ = f32[2,32,256]{2,1,0:T(8,128)S(1)} collective-permute-done((f32[2,32,256]{2,1,0:T(8,128)}, f32[2,32,256]{2,1,0:T(8,128)S(1)}, u32[]{:S(2)}, u32[]{:S(2)}) %collective-permute-start.11) | collective-permute-done | bytes 65568 | tf_op jit(solution)/shard_map/ppermute | solution.py:40
  149.1 3.1 %shard_map.78 = (f32[32,2,512]{2,1,0:T(2,128)}, f32[4,64,384]{2,1,0:T(8,128)}, f32[4,64,384]{2,1,0:T(8,128)}) custom-call(s32[4]{0:T(128)} %pad_add_fusion.ids_ref, f32[2,32,256]{2,1,0:T(8,128)} %get-tuple-element.54.refs_0_, f32[2,32,256]{2,1,0:T(8,128)} %copy-done.21, f32[2,32,256]{2,1,0:T(8,128)} %copy-done.22, f32[2,32,256]{2,1,0:T(8,128)} %copy-done.23, ...), custom_call_target="tpu_custom_call" | custom-call | tf_op jit(solution)/shard_map/pallas_call | solution.py:400
  152.3 2.5 %collective-permute-start.22 = (f32[4,64,384]{2,1,0:T(8,128)}, f32[4,64,384]{2,1,0:T(8,128)S(1)}, u32[]{:S(2)}, u32[]{:S(2)}) collective-permute-start(f32[4,64,384]{2,1,0:T(8,128)} %get-tuple-element.75), channel_id=1, source_target_pairs={{0,4},{4,0},{8,12},{12,8},{16,20},{20,16},{24,28},{28,24},{32,36},... | collective-permute-start | bytes 1179656 | tf_op jit(solution)/shard_map/ppermute | solution.py:40
  154.8 1.6 collective-permute-done.22
  156.3 1.1 add.40
  158.0 2.8 %collective-permute-start.23 = (f32[64,384]{1,0:T(8,128)S(1)}, f32[64,384]{1,0:T(8,128)S(1)}, u32[]{:S(2)}, u32[]{:S(2)}) collective-permute-start(f32[64,384]{1,0:T(8,128)S(1)} %get-tuple-element.80), channel_id=1, source_target_pairs={{0,1},{1,0},{2,3},{3,2},{4,5},{5,4},{6,7},{7,6},{8,9},{9,8},{10,11... | collective-permute-start | bytes 294920 | tf_op jit(solution)/shard_map/ppermute | solution.py:38
  160.8 3.4 %collective-permute-done.25 = f32[64,384]{1,0:T(8,128)S(1)} collective-permute-done((f32[64,384]{1,0:T(8,128)S(1)}, f32[64,384]{1,0:T(8,128)S(1)}, u32[]{:S(2)}, u32[]{:S(2)}) %collective-permute-start.25) | collective-permute-done | bytes 98336 | tf_op jit(solution)/shard_map/ppermute | solution.py:38
  164.2 0.9 collective-permute-done.23
  165.5 3.0 %collective-permute-start.26 = (f32[64,384]{1,0:T(8,128)S(1)}, f32[64,384]{1,0:T(8,128)S(1)}, u32[]{:S(2)}, u32[]{:S(2)}) collective-permute-start(f32[64,384]{1,0:T(8,128)S(1)} %fusion.1), channel_id=1, source_target_pairs={{0,8},{4,12},{8,0},{12,4},{16,24},{20,28},{24,16},{28,20},{32,40},... | collective-permute-start | bytes 294920 | tf_op jit(solution)/shard_map/ppermute | solution.py:40
  168.5 2.9 %collective-permute-done.28 = f32[64,384]{1,0:T(8,128)S(1)} collective-permute-done((f32[64,384]{1,0:T(8,128)S(1)}, f32[64,384]{1,0:T(8,128)S(1)}, u32[]{:S(2)}, u32[]{:S(2)}) %collective-permute-start.28) | collective-permute-done | bytes 98336 | tf_op jit(solution)/shard_map/ppermute | solution.py:40
  171.9 1.0 collective-permute-start.31
  173.3 1.9 collective-permute-start.29
  175.2 1.4 collective-permute-done.31
  176.6 1.2 collective-permute-done.30
  178.3 0.7 collective-permute-start.34
  179.0 0.6 collective-permute-start.33
  179.6 2.0 collective-permute-start.32
  181.6 2.5 %collective-permute-done.34.s3 = f32[64,384]{1,0:T(8,128)S(1)} collective-permute-done((f32[64,384]{1,0:T(8,128)S(1)}, f32[64,384]{1,0:T(8,128)S(1)}, u32[]{:S(2)}, u32[]{:S(2)}) %collective-permute-start.34) | collective-permute-done | bytes 98336 | tf_op jit(solution)/shard_map/ppermute | solution.py:38
  184.7 5.8 %collective-permute-start.35 = (f32[4,64,384]{2,1,0:T(8,128)S(1)}, f32[4,64,384]{2,1,0:T(8,128)S(1)}, u32[]{:S(2)}, u32[]{:S(2)}) collective-permute-start(f32[4,64,384]{2,1,0:T(8,128)S(1)} %pad_maximum_fusion), channel_id=1, source_target_pairs={{0,4},{4,0},{8,12},{12,8},{16,20},{20,16},{24,28},{28,24},{32,36},... | collective-permute-start | bytes 1179656 | tf_op jit(solution)/shard_map/ppermute | solution.py:40
  190.5 1.6 reshape.47
  192.2 0.8 copy-done.6
  192.9 16.9 %shard_map.79 = f32[512,512]{1,0:T(8,128)} custom-call(s32[4]{0:T(128)} %pad_add_fusion.ids_ref, f32[64,384]{1,0:T(8,128)} %copy-done.5, f32[64,384]{1,0:T(8,128)} %copy-done.9, f32[64,384]{1,0:T(8,128)} %copy-done.8, f32[64,384]{1,0:T(8,128)} %copy-done.7, f32[4,64,384]{2,1,0:T(8,128)} %copy-done.6), custom_call_target="tpu_custom_call" | custom-call | tf_op jit(solution)/shard_map/pallas_call | solution.py:423
  (77 shorter events, 4.6 us)
Async XLA Ops:
  1.4 11.5 %collective-permute-start.1 = (f32[16,512]{1,0:T(8,128)S(1)}, f32[16,512]{1,0:T(8,128)S(1)}, u32[]{:S(2)}, u32[]{:S(2)}) collective-permute-start(f32[16,512]{1,0:T(8,128)S(1)} %get-tuple-element.76), channel_id=1, source_target_pairs={{1,0},{2,1},{3,2},{4,3},{5,4},{6,5},{7,6},{8,7},{9,8},{10,9},{11,1... | collective-permute-start | bytes 98312 | tf_op jit(solution)/shard_map/ppermute | solution.py:339
  8.5 6.4 %collective-permute-start = (f32[16,512]{1,0:T(8,128)S(1)}, f32[16,512]{1,0:T(8,128)S(1)}, u32[]{:S(2)}, u32[]{:S(2)}) collective-permute-start(f32[16,512]{1,0:T(8,128)S(1)} %get-tuple-element.77), channel_id=1, source_target_pairs={{0,1},{1,2},{2,3},{3,4},{4,5},{5,6},{6,7},{7,8},{8,9},{9,10},{10,1... | collective-permute-start | bytes 98312 | tf_op jit(solution)/shard_map/ppermute | solution.py:338
  13.0 1.9 copy-start.16
  14.9 0.6 copy-start.17
  24.3 25.0 %collective-permute-start.12 = (f32[4,2,4,32,256]{4,3,2,1,0:T(8,128)}, f32[4,2,4,32,256]{4,3,2,1,0:T(8,128)S(1)}, u32[]{:S(2)}, u32[]{:S(2)}) collective-permute-start(f32[4,2,4,32,256]{4,3,2,1,0:T(8,128)} %bitcast.43), channel_id=1, source_target_pairs={{0,8},{4,12},{8,0},{12,4},{16,24},{20,28},{24,16},{28,20},{32,40},... | collective-permute-start | bytes 3145736 | tf_op jit(solution)/shard_map/ppermute | solution.py:40
  25.9 47.7 %collective-permute-start.13 = (f32[4,2,4,32,256]{4,3,2,1,0:T(8,128)}, f32[4,2,4,32,256]{4,3,2,1,0:T(8,128)}, u32[]{:S(2)}, u32[]{:S(2)}) collective-permute-start(f32[4,2,4,32,256]{4,3,2,1,0:T(8,128)} %bitcast.42), channel_id=1, source_target_pairs={{0,16},{4,20},{8,24},{12,28},{16,0},{20,4},{24,8},{28,12},{32,48},... | collective-permute-start | bytes 3145736 | tf_op jit(solution)/shard_map/ppermute | solution.py:40
  28.3 47.4 %collective-permute-start.14 = (f32[4,2,4,32,256]{4,3,2,1,0:T(8,128)}, f32[4,2,4,32,256]{4,3,2,1,0:T(8,128)}, u32[]{:S(2)}, u32[]{:S(2)}) collective-permute-start(f32[4,2,4,32,256]{4,3,2,1,0:T(8,128)} %bitcast.41), channel_id=1, source_target_pairs={{0,24},{4,28},{8,16},{12,20},{16,8},{20,12},{24,0},{28,4},{32,56},... | collective-permute-start | bytes 3145736 | tf_op jit(solution)/shard_map/ppermute | solution.py:40
  37.4 45.2 %collective-permute-start.2 = (f32[4,4,2,32,256]{4,3,2,1,0:T(8,128)}, f32[4,4,2,32,256]{4,3,2,1,0:T(8,128)S(1)}, u32[]{:S(2)}, u32[]{:S(2)}) collective-permute-start(f32[4,4,2,32,256]{4,3,2,1,0:T(8,128)} %bitcast.40), channel_id=1, source_target_pairs={{0,1},{1,0},{2,3},{3,2},{4,5},{5,4},{6,7},{7,6},{8,9},{9,8},{10,11... | collective-permute-start | bytes 3145736 | tf_op jit(solution)/shard_map/ppermute | solution.py:38
  37.4 49.7 %collective-permute-start.3 = (f32[4,4,2,32,256]{4,3,2,1,0:T(8,128)}, f32[4,4,2,32,256]{4,3,2,1,0:T(8,128)S(1)}, u32[]{:S(2)}, u32[]{:S(2)}) collective-permute-start(f32[4,4,2,32,256]{4,3,2,1,0:T(8,128)} %bitcast.39), channel_id=1, source_target_pairs={{0,2},{1,3},{2,0},{3,1},{4,6},{5,7},{6,4},{7,5},{8,10},{9,11},{10,... | collective-permute-start | bytes 3145736 | tf_op jit(solution)/shard_map/ppermute | solution.py:38
  49.3 26.4 %copy-start.1 = (f32[4,2,4,32,256]{4,3,2,1,0:T(8,128)}, f32[4,2,4,32,256]{4,3,2,1,0:T(8,128)S(1)}, u32[]{:S(2)}) copy-start(f32[4,2,4,32,256]{4,3,2,1,0:T(8,128)S(1)} %collective-permute-done.12.refs_1_) | copy-start | bytes 3145732
  49.3 47.2 %collective-permute-start.4 = (f32[4,4,2,32,256]{4,3,2,1,0:T(8,128)}, f32[4,4,2,32,256]{4,3,2,1,0:T(8,128)}, u32[]{:S(2)}, u32[]{:S(2)}) collective-permute-start(f32[4,4,2,32,256]{4,3,2,1,0:T(8,128)} %bitcast.38), channel_id=1, source_target_pairs={{0,3},{1,2},{2,1},{3,0},{4,7},{5,6},{6,5},{7,4},{8,11},{9,10},{10,... | collective-permute-start | bytes 3145736 | tf_op jit(solution)/shard_map/ppermute | solution.py:38
  80.4 23.2 %collective-permute-start.15 = (f32[2,4,4,32,256]{4,3,2,1,0:T(8,128)}, f32[2,4,4,32,256]{4,3,2,1,0:T(8,128)S(1)}, u32[]{:S(2)}, u32[]{:S(2)}) collective-permute-start(f32[2,4,4,32,256]{4,3,2,1,0:T(8,128)} %get-tuple-element.64), channel_id=1, source_target_pairs={{0,4},{4,0},{8,12},{12,8},{16,20},{20,16},{24,28},{28,24},{32,36},... | collective-permute-start | bytes 3145736 | tf_op jit(solution)/shard_map/ppermute | solution.py:40
  82.5 14.0 %copy-start = (f32[4,4,2,32,256]{4,3,2,1,0:T(8,128)}, f32[4,4,2,32,256]{4,3,2,1,0:T(8,128)S(1)}, u32[]{:S(2)}) copy-start(f32[4,4,2,32,256]{4,3,2,1,0:T(8,128)S(1)} %collective-permute-done.2.refs_1_) | copy-start | bytes 3145732
  87.1 9.4 %copy-start.2 = (f32[4,4,2,32,256]{4,3,2,1,0:T(8,128)}, f32[4,4,2,32,256]{4,3,2,1,0:T(8,128)S(1)}, u32[]{:S(2)}) copy-start(f32[4,4,2,32,256]{4,3,2,1,0:T(8,128)S(1)} %collective-permute-done.3.refs_2_) | copy-start | bytes 3145732
  101.2 9.9 %collective-permute-start.5 = (f32[2,4,4,32,256]{4,3,2,1,0:T(8,128)}, f32[2,4,4,32,256]{4,3,2,1,0:T(8,128)S(1)}, u32[]{:S(2)}, u32[]{:S(2)}) collective-permute-start(f32[2,4,4,32,256]{4,3,2,1,0:T(8,128)} %get-tuple-element.49), channel_id=1, source_target_pairs={{0,4},{4,0},{8,12},{12,8},{16,20},{20,16},{24,28},{28,24},{32,36},... | collective-permute-start | bytes 3145736 | tf_op jit(solution)/shard_map/ppermute | solution.py:40
  103.5 1.0 copy-start.3
  107.2 10.4 %collective-permute-start.16 = (f32[2,4,32,256]{3,2,1,0:T(8,128)}, f32[2,4,32,256]{3,2,1,0:T(8,128)S(1)}, u32[]{:S(2)}, u32[]{:S(2)}) collective-permute-start(f32[2,4,32,256]{3,2,1,0:T(8,128)} %get-tuple-element.66), channel_id=1, source_target_pairs={{0,32},{4,36},{8,40},{12,44},{16,48},{20,52},{24,56},{28,60},{32,0... | collective-permute-start | bytes 786440 | tf_op jit(solution)/shard_map/ppermute | solution.py:40
  107.5 14.9 %collective-permute-start.17 = (f32[2,4,32,256]{3,2,1,0:T(8,128)}, f32[2,4,32,256]{3,2,1,0:T(8,128)S(1)}, u32[]{:S(2)}, u32[]{:S(2)}) collective-permute-start(f32[2,4,32,256]{3,2,1,0:T(8,128)} %get-tuple-element.67), channel_id=1, source_target_pairs={{0,64},{4,68},{8,72},{12,76},{16,80},{20,84},{24,88},{28,92},{32,9... | collective-permute-start | bytes 786440 | tf_op jit(solution)/shard_map/ppermute | solution.py:40
  110.1 14.3 %collective-permute-start.18 = (f32[2,4,32,256]{3,2,1,0:T(8,128)}, f32[2,4,32,256]{3,2,1,0:T(8,128)S(1)}, u32[]{:S(2)}, u32[]{:S(2)}) collective-permute-start(f32[2,4,32,256]{3,2,1,0:T(8,128)} %get-tuple-element.68), channel_id=1, source_target_pairs={{0,96},{4,100},{8,104},{12,108},{16,112},{20,116},{24,120},{28,124... | collective-permute-start | bytes 786440 | tf_op jit(solution)/shard_map/ppermute | solution.py:40
  111.1 1.0 copy-start.4
  114.8 16.3 %collective-permute-start.6 = (f32[2,4,32,256]{3,2,1,0:T(8,128)}, f32[2,4,32,256]{3,2,1,0:T(8,128)S(1)}, u32[]{:S(2)}, u32[]{:S(2)}) collective-permute-start(f32[2,4,32,256]{3,2,1,0:T(8,128)} %get-tuple-element.51), channel_id=1, source_target_pairs={{0,32},{4,36},{8,40},{12,44},{16,48},{20,52},{24,56},{28,60},{32,0... | collective-permute-start | bytes 786440 | tf_op jit(solution)/shard_map/ppermute | solution.py:40
  114.8 18.9 %collective-permute-start.7 = (f32[2,4,32,256]{3,2,1,0:T(8,128)}, f32[2,4,32,256]{3,2,1,0:T(8,128)S(1)}, u32[]{:S(2)}, u32[]{:S(2)}) collective-permute-start(f32[2,4,32,256]{3,2,1,0:T(8,128)} %get-tuple-element.52), channel_id=1, source_target_pairs={{0,64},{4,68},{8,72},{12,76},{16,80},{20,84},{24,88},{28,92},{32,9... | collective-permute-start | bytes 786440 | tf_op jit(solution)/shard_map/ppermute | solution.py:40
  117.6 6.8 %copy-start.12 = (f32[2,4,32,256]{3,2,1,0:T(8,128)}, f32[2,4,32,256]{3,2,1,0:T(8,128)S(1)}, u32[]{:S(2)}) copy-start(f32[2,4,32,256]{3,2,1,0:T(8,128)S(1)} %collective-permute-done.16.refs_1_) | copy-start | bytes 786436
  117.6 18.0 %collective-permute-start.8 = (f32[2,4,32,256]{3,2,1,0:T(8,128)}, f32[2,4,32,256]{3,2,1,0:T(8,128)S(1)}, u32[]{:S(2)}, u32[]{:S(2)}) collective-permute-start(f32[2,4,32,256]{3,2,1,0:T(8,128)} %get-tuple-element.53), channel_id=1, source_target_pairs={{0,96},{4,100},{8,104},{12,108},{16,112},{20,116},{24,120},{28,124... | collective-permute-start | bytes 786440 | tf_op jit(solution)/shard_map/ppermute | solution.py:40
  122.4 2.1 copy-start.14
  124.4 0.7 copy-start.15
  127.2 16.5 %collective-permute-start.19 = (f32[2,32,256]{2,1,0:T(8,128)}, f32[2,32,256]{2,1,0:T(8,128)S(1)}, u32[]{:S(2)}, u32[]{:S(2)}) collective-permute-start(f32[2,32,256]{2,1,0:T(8,128)} %get-tuple-element.70), channel_id=1, source_target_pairs={{0,1},{1,0},{2,3},{3,2},{4,5},{5,4},{6,7},{7,6},{8,9},{9,8},{10,11... | collective-permute-start | bytes 196616 | tf_op jit(solution)/shard_map/ppermute | solution.py:38
  127.2 16.5 %collective-permute-start.20 = (f32[2,32,256]{2,1,0:T(8,128)}, f32[2,32,256]{2,1,0:T(8,128)S(1)}, u32[]{:S(2)}, u32[]{:S(2)}) collective-permute-start(f32[2,32,256]{2,1,0:T(8,128)} %get-tuple-element.71), channel_id=1, source_target_pairs={{0,2},{1,3},{2,0},{3,1},{4,6},{5,7},{6,4},{7,5},{8,10},{9,11},{10,... | collective-permute-start | bytes 196616 | tf_op jit(solution)/shard_map/ppermute | solution.py:38
  131.0 4.7 %copy-start.10 = (f32[2,4,32,256]{3,2,1,0:T(8,128)}, f32[2,4,32,256]{3,2,1,0:T(8,128)S(1)}, u32[]{:S(2)}) copy-start(f32[2,4,32,256]{3,2,1,0:T(8,128)S(1)} %collective-permute-done.6.refs_1_) | copy-start | bytes 786436
  131.0 12.6 %collective-permute-start.21 = (f32[2,32,256]{2,1,0:T(8,128)}, f32[2,32,256]{2,1,0:T(8,128)S(1)}, u32[]{:S(2)}, u32[]{:S(2)}) collective-permute-start(f32[2,32,256]{2,1,0:T(8,128)} %get-tuple-element.72), channel_id=1, source_target_pairs={{0,3},{1,2},{2,1},{3,0},{4,7},{5,6},{6,5},{7,4},{8,11},{9,10},{10,... | collective-permute-start | bytes 196616 | tf_op jit(solution)/shard_map/ppermute | solution.py:38
  133.6 2.0 copy-start.11
  135.7 0.7 copy-start.13
  138.3 5.3 %collective-permute-start.9 = (f32[2,32,256]{2,1,0:T(8,128)}, f32[2,32,256]{2,1,0:T(8,128)S(1)}, u32[]{:S(2)}, u32[]{:S(2)}) collective-permute-start(f32[2,32,256]{2,1,0:T(8,128)} %get-tuple-element.55), channel_id=1, source_target_pairs={{0,8},{4,12},{8,0},{12,4},{16,24},{20,28},{24,16},{28,20},{32,40},... | collective-permute-start | bytes 196616 | tf_op jit(solution)/shard_map/ppermute | solution.py:40
  139.5 6.6 %collective-permute-start.10 = (f32[2,32,256]{2,1,0:T(8,128)}, f32[2,32,256]{2,1,0:T(8,128)S(1)}, u32[]{:S(2)}, u32[]{:S(2)}) collective-permute-start(f32[2,32,256]{2,1,0:T(8,128)} %get-tuple-element.56), channel_id=1, source_target_pairs={{0,16},{4,20},{8,24},{12,28},{16,0},{20,4},{24,8},{28,12},{32,48},... | collective-permute-start | bytes 196616 | tf_op jit(solution)/shard_map/ppermute | solution.py:40
  143.6 4.9 %copy-start.18 = (f32[2,32,256]{2,1,0:T(8,128)}, f32[2,32,256]{2,1,0:T(8,128)S(1)}, u32[]{:S(2)}) copy-start(f32[2,32,256]{2,1,0:T(8,128)S(1)} %collective-permute-done.19.refs_5_) | copy-start | bytes 196612
  143.6 4.9 %collective-permute-start.11 = (f32[2,32,256]{2,1,0:T(8,128)}, f32[2,32,256]{2,1,0:T(8,128)S(1)}, u32[]{:S(2)}, u32[]{:S(2)}) collective-permute-start(f32[2,32,256]{2,1,0:T(8,128)} %get-tuple-element.57), channel_id=1, source_target_pairs={{0,24},{4,28},{8,16},{12,20},{16,8},{20,12},{24,0},{28,4},{32,56},... | collective-permute-start | bytes 196616 | tf_op jit(solution)/shard_map/ppermute | solution.py:40
  143.7 4.9 %copy-start.19 = (f32[2,32,256]{2,1,0:T(8,128)}, f32[2,32,256]{2,1,0:T(8,128)S(1)}, u32[]{:S(2)}) copy-start(f32[2,32,256]{2,1,0:T(8,128)S(1)} %collective-permute-done.20.refs_6_) | copy-start | bytes 196612
  143.7 4.8 %copy-start.20 = (f32[2,32,256]{2,1,0:T(8,128)}, f32[2,32,256]{2,1,0:T(8,128)S(1)}, u32[]{:S(2)}) copy-start(f32[2,32,256]{2,1,0:T(8,128)S(1)} %collective-permute-done.21.refs_7_) | copy-start | bytes 196612
  143.7 4.8 %copy-start.21 = (f32[2,32,256]{2,1,0:T(8,128)}, f32[2,32,256]{2,1,0:T(8,128)S(1)}, u32[]{:S(2)}) copy-start(f32[2,32,256]{2,1,0:T(8,128)S(1)} %collective-permute-done.9.refs_1_) | copy-start | bytes 196612
  146.2 2.3 %copy-start.22 = (f32[2,32,256]{2,1,0:T(8,128)}, f32[2,32,256]{2,1,0:T(8,128)S(1)}, u32[]{:S(2)}) copy-start(f32[2,32,256]{2,1,0:T(8,128)S(1)} %collective-permute-done.10.refs_2_) | copy-start | bytes 196612
  148.5 0.6 copy-start.23
  152.3 4.1 %collective-permute-start.22 = (f32[4,64,384]{2,1,0:T(8,128)}, f32[4,64,384]{2,1,0:T(8,128)S(1)}, u32[]{:S(2)}, u32[]{:S(2)}) collective-permute-start(f32[4,64,384]{2,1,0:T(8,128)} %get-tuple-element.75), channel_id=1, source_target_pairs={{0,4},{4,0},{8,12},{12,8},{16,20},{20,16},{24,28},{28,24},{32,36},... | collective-permute-start | bytes 1179656 | tf_op jit(solution)/shard_map/ppermute | solution.py:40
  157.4 6.8 %collective-permute-start.25 = (f32[64,384]{1,0:T(8,128)S(1)}, f32[64,384]{1,0:T(8,128)S(1)}, u32[]{:S(2)}, u32[]{:S(2)}) collective-permute-start(f32[64,384]{1,0:T(8,128)S(1)} %get-tuple-element.78), channel_id=1, source_target_pairs={{0,3},{1,2},{2,1},{3,0},{4,7},{5,6},{6,5},{7,4},{8,11},{9,10},{10,... | collective-permute-start | bytes 294920 | tf_op jit(solution)/shard_map/ppermute | solution.py:38
  158.0 6.2 %collective-permute-start.24 = (f32[64,384]{1,0:T(8,128)S(1)}, f32[64,384]{1,0:T(8,128)S(1)}, u32[]{:S(2)}, u32[]{:S(2)}) collective-permute-start(f32[64,384]{1,0:T(8,128)S(1)} %get-tuple-element.79), channel_id=1, source_target_pairs={{0,2},{1,3},{2,0},{3,1},{4,6},{5,7},{6,4},{7,5},{8,10},{9,11},{10,... | collective-permute-start | bytes 294920 | tf_op jit(solution)/shard_map/ppermute | solution.py:38
  158.0 7.1 %collective-permute-start.23 = (f32[64,384]{1,0:T(8,128)S(1)}, f32[64,384]{1,0:T(8,128)S(1)}, u32[]{:S(2)}, u32[]{:S(2)}) collective-permute-start(f32[64,384]{1,0:T(8,128)S(1)} %get-tuple-element.80), channel_id=1, source_target_pairs={{0,1},{1,0},{2,3},{3,2},{4,5},{5,4},{6,7},{7,6},{8,9},{9,8},{10,11... | collective-permute-start | bytes 294920 | tf_op jit(solution)/shard_map/ppermute | solution.py:38
  165.1 6.2 %collective-permute-start.28 = (f32[64,384]{1,0:T(8,128)S(1)}, f32[64,384]{1,0:T(8,128)S(1)}, u32[]{:S(2)}, u32[]{:S(2)}) collective-permute-start(f32[64,384]{1,0:T(8,128)S(1)} %fusion.1), channel_id=1, source_target_pairs={{0,24},{4,28},{8,16},{12,20},{16,8},{20,12},{24,0},{28,4},{32,56},... | collective-permute-start | bytes 294920 | tf_op jit(solution)/shard_map/ppermute | solution.py:40
  165.2 6.1 %collective-permute-start.27 = (f32[64,384]{1,0:T(8,128)S(1)}, f32[64,384]{1,0:T(8,128)S(1)}, u32[]{:S(2)}, u32[]{:S(2)}) collective-permute-start(f32[64,384]{1,0:T(8,128)S(1)} %fusion.1), channel_id=1, source_target_pairs={{0,16},{4,20},{8,24},{12,28},{16,0},{20,4},{24,8},{28,12},{32,48},... | collective-permute-start | bytes 294920 | tf_op jit(solution)/shard_map/ppermute | solution.py:40
  165.5 6.4 %collective-permute-start.26 = (f32[64,384]{1,0:T(8,128)S(1)}, f32[64,384]{1,0:T(8,128)S(1)}, u32[]{:S(2)}, u32[]{:S(2)}) collective-permute-start(f32[64,384]{1,0:T(8,128)S(1)} %fusion.1), channel_id=1, source_target_pairs={{0,8},{4,12},{8,0},{12,4},{16,24},{20,28},{24,16},{28,20},{32,40},... | collective-permute-start | bytes 294920 | tf_op jit(solution)/shard_map/ppermute | solution.py:40
  171.9 4.8 %collective-permute-start.31 = (f32[64,384]{1,0:T(8,128)S(1)}, f32[64,384]{1,0:T(8,128)S(1)}, u32[]{:S(2)}, u32[]{:S(2)}) collective-permute-start(f32[64,384]{1,0:T(8,128)S(1)} %add_add_fusion.1), channel_id=1, source_target_pairs={{0,96},{4,100},{8,104},{12,108},{16,112},{20,116},{24,120},{28,124... | collective-permute-start | bytes 294920 | tf_op jit(solution)/shard_map/ppermute | solution.py:40
  172.8 5.0 %collective-permute-start.30 = (f32[64,384]{1,0:T(8,128)S(1)}, f32[64,384]{1,0:T(8,128)S(1)}, u32[]{:S(2)}, u32[]{:S(2)}) collective-permute-start(f32[64,384]{1,0:T(8,128)S(1)} %add_add_fusion.1), channel_id=1, source_target_pairs={{0,64},{4,68},{8,72},{12,76},{16,80},{20,84},{24,88},{28,92},{32,9... | collective-permute-start | bytes 294920 | tf_op jit(solution)/shard_map/ppermute | solution.py:40
  173.3 4.9 %collective-permute-start.29 = (f32[64,384]{1,0:T(8,128)S(1)}, f32[64,384]{1,0:T(8,128)S(1)}, u32[]{:S(2)}, u32[]{:S(2)}) collective-permute-start(f32[64,384]{1,0:T(8,128)S(1)} %add_add_fusion.1), channel_id=1, source_target_pairs={{0,32},{4,36},{8,40},{12,44},{16,48},{20,52},{24,56},{28,60},{32,0... | collective-permute-start | bytes 294920 | tf_op jit(solution)/shard_map/ppermute | solution.py:40
  178.3 13.9 %copy-start.5 = (f32[64,384]{1,0:T(8,128)}, f32[64,384]{1,0:T(8,128)S(1)}, u32[]{:S(2)}) copy-start(f32[64,384]{1,0:T(8,128)S(1)} %add_add_fusion.s0) | copy-start | bytes 294916
  178.3 5.8 %collective-permute-start.34 = (f32[64,384]{1,0:T(8,128)S(1)}, f32[64,384]{1,0:T(8,128)S(1)}, u32[]{:S(2)}, u32[]{:S(2)}) collective-permute-start(f32[64,384]{1,0:T(8,128)S(1)} %add_add_fusion.s0), channel_id=1, source_target_pairs={{0,3},{1,2},{2,1},{3,0},{4,7},{5,6},{6,5},{7,4},{8,11},{9,10},{10,... | collective-permute-start | bytes 294920 | tf_op jit(solution)/shard_map/ppermute | solution.py:38
  179.0 5.2 %collective-permute-start.33 = (f32[64,384]{1,0:T(8,128)S(1)}, f32[64,384]{1,0:T(8,128)S(1)}, u32[]{:S(2)}, u32[]{:S(2)}) collective-permute-start(f32[64,384]{1,0:T(8,128)S(1)} %add_add_fusion.s0), channel_id=1, source_target_pairs={{0,2},{1,3},{2,0},{3,1},{4,6},{5,7},{6,4},{7,5},{8,10},{9,11},{10,... | collective-permute-start | bytes 294920 | tf_op jit(solution)/shard_map/ppermute | solution.py:38
  179.6 5.1 %collective-permute-start.32 = (f32[64,384]{1,0:T(8,128)S(1)}, f32[64,384]{1,0:T(8,128)S(1)}, u32[]{:S(2)}, u32[]{:S(2)}) collective-permute-start(f32[64,384]{1,0:T(8,128)S(1)} %add_add_fusion.s0), channel_id=1, source_target_pairs={{0,1},{1,0},{2,3},{3,2},{4,5},{5,4},{6,7},{7,6},{8,9},{9,8},{10,11... | collective-permute-start | bytes 294920 | tf_op jit(solution)/shard_map/ppermute | solution.py:38
  184.1 8.0 %copy-start.7 = (f32[64,384]{1,0:T(8,128)}, f32[64,384]{1,0:T(8,128)S(1)}, u32[]{:S(2)}) copy-start(f32[64,384]{1,0:T(8,128)S(1)} %collective-permute-done.34.s3) | copy-start | bytes 294916
  184.1 8.0 %copy-start.8 = (f32[64,384]{1,0:T(8,128)}, f32[64,384]{1,0:T(8,128)S(1)}, u32[]{:S(2)}) copy-start(f32[64,384]{1,0:T(8,128)S(1)} %collective-permute-done.33.s2) | copy-start | bytes 294916
  184.7 7.5 %copy-start.9 = (f32[64,384]{1,0:T(8,128)}, f32[64,384]{1,0:T(8,128)S(1)}, u32[]{:S(2)}) copy-start(f32[64,384]{1,0:T(8,128)S(1)} %collective-permute-done.32.s1) | copy-start | bytes 294916
  184.7 7.4 %collective-permute-start.35 = (f32[4,64,384]{2,1,0:T(8,128)S(1)}, f32[4,64,384]{2,1,0:T(8,128)S(1)}, u32[]{:S(2)}, u32[]{:S(2)}) collective-permute-start(f32[4,64,384]{2,1,0:T(8,128)S(1)} %pad_maximum_fusion), channel_id=1, source_target_pairs={{0,4},{4,0},{8,12},{12,8},{16,20},{20,16},{24,28},{28,24},{32,36},... | collective-permute-start | bytes 1179656 | tf_op jit(solution)/shard_map/ppermute | solution.py:40
  192.2 0.8 copy-start.6
where the time goes:
time: 211 us; the launch traced here: 210 us
  waiting for transfers between devices  75.7 us (36%)
  starting transfers between devices  61.9 us (29%)
  Pallas kernels  61.8 us (29%)
  local copies, waits for them, and re-layouts  7.84 us (4%)
    ppermute x22, waiting for transfers between devices, to_partner(): return lax.ppermute(value, 'tm', [(i, i ^ step) for i in range(32)])  52.4 us
    ppermute x22, starting transfers between devices, to_partner(): return lax.ppermute(value, 'tm', [(i, i ^ step) for i in range(32)])  36.5 us
    ppermute x12, waiting for transfers between devices, to_partner(): return lax.ppermute(value, 'grp', [(i, i ^ delta) for i in range(4)])  21.4 us
    pallas_call x2, Pallas kernels, on_device(): pl.pallas_call(functools.partial(local_kernel, half == 0), grid=(1,), in_...  17.9 us
    pallas_call x1, Pallas kernels, on_device(): pl.pallas_call(cholesky_kernel, in_specs=[SMEM] + [WHOLE] * 5, out_specs=...  16.9 us
    ppermute x12, starting transfers between devices, to_partner(): return lax.ppermute(value, 'grp', [(i, i ^ delta) for i in range(4)])  16.5 us
    pallas_call x2, Pallas kernels, first_stage(): pl.pallas_call(functools.partial(first_kernel, bit, core_dim), grid=(4,),...  9.28 us
    ppermute x1, starting transfers between devices, on_device(): nxt = lax.ppermute(series[:HALF], ('tm', 'grp'), [(b, a) for a, b in up])  7.03 us
  transfers between devices with their start and end apart: 36, of which 22 were waited for; matrix products, arithmetic and copies ran while one was open for 1% of the time, Pallas kernels for 16%

commit v1 on v0

--- a/solution.py
+++ b/solution.py
@@ -22,6 +22,14 @@
 VMEM = pltpu.VMEM
 WHOLE = pl.BlockSpec(memory_space=VMEM)
 SMEM = pl.BlockSpec(memory_space=pltpu.SMEM)
+
+
+def room(mib):
+    return pltpu.CompilerParams(vmem_limit_bytes=mib << 20)
+
+
+def on_chip(values):
+    return [pltpu.with_memory_space_constraint(v, pltpu.VMEM) for v in values]
 
 
 def np_hadamard(order):
@@ -85,13 +93,14 @@
                         b_ref[s, y, c, z ^ (2 * h + low)] = column(4 + h, s, low)
 
 
-def local_kernel(by_z, x_ref, prev_ref, next_ref, band_ref, had_ref, flip_ref, *refs):
+def local_kernel(half, x_ref, prev_ref, next_ref, band_ref, had_ref, flip_ref, *refs):
     outs, mid_ref = refs[:4], refs[4]
+    cols = slice(256 * half, 256 * half + 256)
     for b in range(16):
         if b == 0:
-            window = jnp.concatenate([prev_ref[...], x_ref[0 : BLK + HALF]], 0)
+            window = jnp.concatenate([prev_ref[:, cols], x_ref[0 : BLK + HALF]], 0)
         elif b == 15:
-            window = jnp.concatenate([x_ref[b * BLK - HALF :], next_ref[...]], 0)
+            window = jnp.concatenate([x_ref[b * BLK - HALF :], next_ref[:, cols]], 0)
         else:
             window = x_ref[b * BLK - HALF : (b + 1) * BLK + HALF]
         high = window.astype(BF16)
@@ -132,7 +141,7 @@
             outs[i % 4][i // 4, pl.ds(at, 8), :] = vals[i]
         return 0
 
-    if by_z:
+    if half == 0:
         for d in range(4):
             lax.fori_loop(0, 8, functools.partial(rows_of_z, d), 0)
     else:
@@ -144,23 +153,22 @@
     return jnp.concatenate([e] * (width // 128), -1) if width > 128 else e
 
 
-def core_kernel(keep_ref, recv_ref, o_ref, *outs):
+def core_kernel(pick, keep_ref, recv_ref, o_ref, *outs):
     for s in range(2):
         for y in range(4):
             for d in range(4):
-                e = sign_of(o_ref[s, y, d], CB, 256)
+                e = sign_of(o_ref[(s, y, *pick(d))], CB, 256)
                 outs[y][s, d] = keep_ref[s, y, d] + e * recv_ref[s, y, d]
 
 
-def core_stage(keep, recv, owners, block):
-    whole = pl.BlockSpec(keep.shape, lambda i: (0,) * 5)
+def core_stage(keep, recv, owners, pick):
     return pl.pallas_call(
-        core_kernel,
-        grid=(1,),
-        in_specs=[whole, whole, pl.BlockSpec(block, lambda i: (0,) * 6)],
-        out_specs=[pl.BlockSpec((2, 4, 32, 256), lambda i: (0,) * 4)] * 4,
-        out_shape=[jax.ShapeDtypeStruct((2, 4, 32, 256), F32)] * 4,
-    )(keep, recv, owners)
+        functools.partial(core_kernel, pick),
+        in_specs=[WHOLE] * 3,
+        out_specs=[WHOLE] * 4,
+        out_shape=[VMEM((2, 4, 32, 256), F32)] * 4,
+        compiler_params=room(12),
+    )(*on_chip([keep, recv]), owners)
 
 
 def merged(parts, owner, bit):
@@ -169,49 +177,45 @@
     return (parts[0] + e0 * parts[1]) + e1 * (parts[2] + e0 * parts[3])
 
 
-def merge_kernel(bit, cut, *refs):
+def merge_kernel(bit, cut, pick, *refs):
     ins, o_ref, outs = refs[:4], refs[4], refs[5:]
     lead = ins[0].shape[1:-2]
     for s in range(2):
         for at in np.ndindex(*lead):
-            value = merged([r[(s, *at)] for r in ins], o_ref[(s, *at)], bit)
+            value = merged([r[(s, *at)] for r in ins], o_ref[(s, *pick(*at))], bit)
             rest = tuple(v for d, v in enumerate(at) if d != cut)
             outs[at[cut]][(s, *rest)] = value
 
 
+def merge_stage(parts, owners, bit, cut, pick):
+    shape = parts[0].shape
+    out = tuple(v for d, v in enumerate(shape) if d != cut + 1)
+    return pl.pallas_call(
+        functools.partial(merge_kernel, bit, cut, pick),
+        in_specs=[WHOLE] * 5,
+        out_specs=[WHOLE] * 4,
+        out_shape=[VMEM(out, F32)] * 4,
+        compiler_params=room(12),
+    )(*on_chip(parts), owners)
+
+
 def first_kernel(bit, core_dim, *refs):
     ins, o_ref, outs = refs[:4], refs[4], refs[5:]
-    lead = ins[0].shape[1:-2]
-    for at in np.ndindex(*lead):
-        parts = [r[(0, *at)] for r in ins]
+    for at in np.ndindex(*ins[0].shape[:-2]):
+        parts = [r[at] for r in ins]
         rest = tuple(v for d, v in enumerate(at) if d != core_dim)
         for s in range(2):
-            outs[at[core_dim]][(s, 0, *rest)] = merged(parts, o_ref[(s, 0, *at)], bit)
+            outs[at[core_dim]][(s, *rest)] = merged(parts, o_ref[(s, *at)], bit)
 
 
 def first_stage(parts, owners, bit, core_dim):
-    lead = parts[0].shape[1:-2]
     return pl.pallas_call(
         functools.partial(first_kernel, bit, core_dim),
-        grid=(4,),
-        in_specs=[pl.BlockSpec((1, *lead, 32, 256), lambda i: (i, 0, 0, 0, 0))] * 4
-        + [pl.BlockSpec((2, 1, *lead, 32, 128), lambda i: (0, i, 0, 0, 0, 0))],
-        out_specs=[pl.BlockSpec((2, 1, 4, 32, 256), lambda i: (0, i, 0, 0, 0))] * 2,
-        out_shape=[jax.ShapeDtypeStruct((2, 4, 4, 32, 256), F32)] * 2,
-    )(*parts, owners)
-
-
-def merge_stage(parts, owners, bit, cut, block):
-    shape = parts[0].shape
-    out = tuple(v for d, v in enumerate(shape) if d != cut + 1)
-    whole = lambda dims: pl.BlockSpec(dims, lambda i: (0,) * len(dims))
-    return pl.pallas_call(
-        functools.partial(merge_kernel, bit, cut),
-        grid=(1,),
-        in_specs=[whole(shape)] * 4 + [pl.BlockSpec(block, lambda i: (0,) * 6)],
-        out_specs=[whole(out)] * 4,
-        out_shape=[jax.ShapeDtypeStruct(out, F32)] * 4,
-    )(*parts, owners)
+        in_specs=[WHOLE] * 5,
+        out_specs=[WHOLE] * 2,
+        out_shape=[VMEM((2, 4, 4, 32, 256), F32)] * 2,
+        compiler_params=room(12),
+    )(*on_chip(parts), owners)
 
 
 def final_kernel(ids_ref, *refs):
@@ -220,7 +224,7 @@
     core, z, me = ids_ref[1], ids_ref[2], ids_ref[3]
     halves = []
     for s in range(2):
-        owner = o_ref[s]
+        owner = o_ref[s, 0, 0, 0]
         parity = owner & me
         parity = parity ^ lax.shift_right_logical(parity, 4)
         parity = parity ^ lax.shift_right_logical(parity, 2)
@@ -343,30 +347,23 @@
         prepare_kernel,
         in_specs=[SMEM, SMEM, WHOLE],
         out_specs=[WHOLE] * 2,
-        out_shape=[
-            jax.ShapeDtypeStruct((BLK, 3 * WIN), BF16),
-            jax.ShapeDtypeStruct((16, BLK), F32),
-        ],
+        out_shape=[VMEM((BLK, 3 * WIN), BF16), VMEM((16, BLK), F32)],
+        compiler_params=room(12),
     )(ids, filter_taps, sign_flips.reshape(32, 128))
+    prev, nxt, bands, flips = on_chip([prev, nxt, bands, flips])
 
     firsts = []
     for half in range(2):
         cut = lambda i, half=half: (0, half)
         out = (16, 64, 256) if half == 0 else (4, 256, 256)
         parts = pl.pallas_call(
-            functools.partial(local_kernel, half == 0),
+            functools.partial(local_kernel, half),
             grid=(1,),
-            in_specs=[
-                pl.BlockSpec((ROWS_DEV, 256), cut),
-                pl.BlockSpec((HALF, 256), cut),
-                pl.BlockSpec((HALF, 256), cut),
-                pl.BlockSpec((BLK, 3 * WIN), lambda i: (0, 0)),
-                pl.BlockSpec((BLK, BLK), lambda i: (0, 0)),
-                pl.BlockSpec((16, BLK), lambda i: (0, 0)),
-            ],
-            out_specs=[pl.BlockSpec(out, lambda i: (0, 0, 0))] * 4,
-            out_shape=[jax.ShapeDtypeStruct(out, F32)] * 4,
+            in_specs=[pl.BlockSpec((ROWS_DEV, 256), cut)] + [WHOLE] * 5,
+            out_specs=[WHOLE] * 4,
+            out_shape=[VMEM(out, F32)] * 4,
             scratch_shapes=[VMEM((16, BLK, 256), F32)],
+            compiler_params=room(24),
         )(series, prev, nxt, bands, had, flips)
         shape = (4, 4, 2, 32, 256) if half == 0 else (4, 2, 4, 32, 256)
         firsts.append([p.reshape(shape) for p in parts])
@@ -378,38 +375,35 @@
         owners_kernel,
         in_specs=[SMEM, WHOLE],
         out_specs=[WHOLE] * 2,
-        out_shape=[
-            jax.ShapeDtypeStruct((2, 4, 4, 2, 32, 128), jnp.int32),
-            jax.ShapeDtypeStruct((2, 4, 2, 4, 32, 128), jnp.int32),
-        ],
+        out_shape=[VMEM((2, 4, 4, 2, 32, 128), jnp.int32), VMEM((2, 4, 2, 4, 32, 128), jnp.int32)],
         scratch_shapes=[VMEM((6, 128, 128), F32)],
+        compiler_params=room(12),
     )(ids, late)
 
-    none = None
-    keep, send = first_stage(a, owners_a, Z0, 1)
-    a = list(core_stage(keep, to_partner(send, "c", 1), owners_a, (2, 4, 4, none, 32, 128)))
+    owners_a, owners_b = on_chip([owners_a, owners_b])
+    keep, send = first_stage(a, owners_a, Z0, 2)
+    a = list(core_stage(keep, to_partner(send, "c", 1), owners_a, lambda x: (x, 0)))
     a = spread(a, "y")
-    keep, send = first_stage(b, owners_b, X0, 0)
-    b = core_stage(keep, to_partner(send, "c", 1), owners_b, (2, 4, none, 4, 32, 128))
+    keep, send = first_stage(b, owners_b, X0, 1)
+    b = core_stage(keep, to_partner(send, "c", 1), owners_b, lambda z: (0, z))
     b = spread(b, "y")
-    a = merge_stage(a, owners_a, Y0, 0, (2, none, 4, none, 32, 128))
+    a = merge_stage(a, owners_a, Y0, 0, lambda x: (0, x, 0))
     a = spread(a, "x")
-    b = merge_stage(b, owners_b, Y0, 0, (2, none, none, 4, 32, 128))
+    b = merge_stage(b, owners_b, Y0, 0, lambda z: (0, 0, z))
     b = spread(b, "z")
 
     sketch, keep, send = pl.pallas_call(
         final_kernel,
-        grid=(1,),
-        in_specs=[SMEM] + [WHOLE] * 8
-        + [pl.BlockSpec((2, none, none, none, 32, 128), lambda i: (0,) * 6)],
+        in_specs=[SMEM] + [WHOLE] * 9,
         out_specs=[WHOLE] * 3,
         out_shape=[
             jax.ShapeDtypeStruct((32, 2, COLS), F32),
-            jax.ShapeDtypeStruct((4, 64, 384), F32),
-            jax.ShapeDtypeStruct((4, 64, 384), F32),
+            VMEM((4, 64, 384), F32),
+            VMEM((4, 64, 384), F32),
         ],
         scratch_shapes=[VMEM((COLS, COLS), F32)],
-    )(ids, *a, *b, owners_a)
+        compiler_params=room(12),
+    )(ids, *on_chip(a), *on_chip(b), owners_a)
     sketch = sketch.reshape(64, COLS)
 
     held = keep + to_partner(send, "c", 1)
@@ -426,7 +420,8 @@
         out_specs=WHOLE,
         out_shape=jax.ShapeDtypeStruct((COLS, COLS), F32),
         scratch_shapes=[VMEM((COLS, COLS), F32)],
-    )(ids, *near, far)
+        compiler_params=room(12),
+    )(ids, *on_chip(near), *on_chip([far]))
     return (sketch, r_factor)
 
 

time: 211 us -> 195 us (0.924)
  Pallas kernels: 61.8 us -> 33 us
  waiting for transfers between devices: 75.7 us -> 89.6 us
    pallas_call x9, Pallas kernels: 39.6 us -> 14 us  [the longest x2 10.3 us: on_device(): pl.pallas_call(functools.partial(local_kernel, half), grid=(1,), in_specs...]
    ppermute x22, waiting for transfers between devices: 52.4 us -> 62.9 us  [to_partner(): return lax.ppermute(value, 'tm', [(i, i ^ step) for i in range(32)])]
    ppermute x12, waiting for transfers between devices: 21.4 us -> 24.7 us  [to_partner(): return lax.ppermute(value, 'grp', [(i, i ^ delta) for i in range(4)])]
    unnamed x48 -> x10, local copies, waits for them, and re-layouts: 5.38 us -> 5.66 us
  transfers between devices with their start and end apart: 36 -> 36, of which waited for: 22 -> 25; matrix products, arithmetic and copies ran while one was open for 1% -> 0% of each run, Pallas kernels for 16% -> 5%
where the time goes in v1:
time: 195 us; the launch traced here: 194 us
  waiting for transfers between devices  89.6 us (46%)
  starting transfers between devices  63.4 us (33%)
  Pallas kernels  33 us (17%)
  local copies, waits for them, and re-layouts  7.21 us (4%)
    ppermute x22, waiting for transfers between devices, to_partner(): return lax.ppermute(value, 'tm', [(i, i ^ step) for i in range(32)])  62.9 us
    ppermute x22, starting transfers between devices, to_partner(): return lax.ppermute(value, 'tm', [(i, i ^ step) for i in range(32)])  38 us
    ppermute x12, waiting for transfers between devices, to_partner(): return lax.ppermute(value, 'grp', [(i, i ^ delta) for i in range(4)])  24.7 us
    ppermute x12, starting transfers between devices, to_partner(): return lax.ppermute(value, 'grp', [(i, i ^ delta) for i in range(4)])  16.4 us
    pallas_call x1, Pallas kernels, on_device(): pl.pallas_call(cholesky_kernel, in_specs=[SMEM] + [WHOLE] * 5, out_specs=...  16.3 us
    pallas_call x2, Pallas kernels, on_device(): pl.pallas_call(functools.partial(local_kernel, half), grid=(1,), in_specs...  10.3 us
    ppermute x1, starting transfers between devices, on_device(): nxt = lax.ppermute(series[:HALF], ('tm', 'grp'), [(b, a) for a, b in up])  7.03 us
    unnamed x10, local copies, waits for them, and re-layouts  5.66 us
  transfers between devices with their start and end apart: 36, of which 25 were waited for; matrix products, arithmetic and copies ran while one was open for 0% of the time, Pallas kernels for 5%

profile of v1, /device:TPU:1, one launch (start us, length us, event | category | flops | bytes accessed | tf_op | source)
XLA Modules:
  0.0 194.2 jit_solution(6459770664876436053)
XLA Ops:
  0.6 0.8 fusion.2
  1.4 7.0 %collective-permute-start.1 = (f32[16,512]{1,0:T(8,128)S(1)}, f32[16,512]{1,0:T(8,128)S(1)}, u32[]{:S(2)}, u32[]{:S(2)}) collective-permute-start(f32[16,512]{1,0:T(8,128)S(1)} %get-tuple-element.76), channel_id=1, source_target_pairs={{1,0},{2,1},{3,2},{4,3},{5,4},{6,5},{7,6},{8,7},{9,8},{10,9},{11,1... | collective-permute-start | bytes 98312 | tf_op jit(solution)/shard_map/ppermute | solution.py:343
  8.5 1.9 collective-permute-start
  10.5 0.7 copy-done.3
  11.2 0.7 copy-done.4
  11.9 1.0 shard_map.68
  12.9 2.0 %collective-permute-done.prev_ref = f32[16,512]{1,0:T(8,128)S(1)} collective-permute-done((f32[16,512]{1,0:T(8,128)S(1)}, f32[16,512]{1,0:T(8,128)S(1)}, u32[]{:S(2)}, u32[]{:S(2)}) %collective-permute-start) | collective-permute-done | bytes 32800 | tf_op jit(solution)/shard_map/ppermute | solution.py:342
  14.9 3.4 %copy-done = f32[4096,512]{1,0:T(8,128)S(1)} copy-done((f32[4096,512]{1,0:T(8,128)S(1)}, f32[4096,512]{1,0:T(8,128)}, u32[]{:S(2)}) %copy-start) | copy-done | bytes 8388632
  18.3 0.9 copy-done.1
  19.2 5.0 %shard_map.70 = (f32[4,256,256]{2,1,0:T(8,128)S(1)}, f32[4,256,256]{2,1,0:T(8,128)S(1)}, f32[4,256,256]{2,1,0:T(8,128)S(1)}, f32[4,256,256]{2,1,0:T(8,128)S(1)}) custom-call(f32[4096,512]{1,0:T(8,128)S(1)} %copy-done, f32[16,512]{1,0:T(8,128)S(1)} %collective-permute-done.prev_ref, f32[16,512]{1,0:T(8,128)S(1)} %collective-permute-done.1.next_ref, ...), custom_call_target="tpu_custom_call" | custom-call | tf_op jit(solution)/shard_map/pallas_call | solution.py:359
  24.2 1.6 collective-permute-start.12
  25.9 2.4 %collective-permute-start.13 = (f32[4,2,4,32,256]{4,3,2,1,0:T(8,128)S(1)}, f32[4,2,4,32,256]{4,3,2,1,0:T(8,128)S(1)}, u32[]{:S(2)}, u32[]{:S(2)}) collective-permute-start(f32[4,2,4,32,256]{4,3,2,1,0:T(8,128)S(1)} %bitcast.42), channel_id=1, source_target_pairs={{0,16},{4,20},{8,24},{12,28},{16,0},{20,4},{24,8},{28,12},{32,48},... | collective-permute-start | bytes 3145736 | tf_op jit(solution)/shard_map/ppermute | solution.py:48
  28.3 5.3 %shard_map.69 = (f32[16,64,256]{2,1,0:T(8,128)S(1)}, f32[16,64,256]{2,1,0:T(8,128)S(1)}, f32[16,64,256]{2,1,0:T(8,128)S(1)}, f32[16,64,256]{2,1,0:T(8,128)S(1)}) custom-call(f32[4096,512]{1,0:T(8,128)S(1)} %copy-done, f32[16,512]{1,0:T(8,128)S(1)} %collective-permute-done.prev_ref, f32[16,512]{1,0:T(8,128)S(1)} %collective-permute-done.1.next_ref, ...), custom_call_target="tpu_custom_call" | custom-call | tf_op jit(solution)/shard_map/pallas_call | solution.py:359
  33.7 4.1 %collective-permute-start.3 = (f32[4,4,2,32,256]{4,3,2,1,0:T(8,128)S(1)}, f32[4,4,2,32,256]{4,3,2,1,0:T(8,128)S(1)}, u32[]{:S(2)}, u32[]{:S(2)}) collective-permute-start(f32[4,4,2,32,256]{4,3,2,1,0:T(8,128)S(1)} %bitcast.39), channel_id=1, source_target_pairs={{0,2},{1,3},{2,0},{3,1},{4,6},{5,7},{6,4},{7,5},{8,10},{9,11},{10,... | collective-permute-start | bytes 3145736 | tf_op jit(solution)/shard_map/ppermute | solution.py:46
  37.8 11.1 %collective-permute-done.12.refs_1_ = f32[4,2,4,32,256]{4,3,2,1,0:T(8,128)S(1)} collective-permute-done((f32[4,2,4,32,256]{4,3,2,1,0:T(8,128)S(1)}, f32[4,2,4,32,256]{4,3,2,1,0:T(8,128)S(1)}, u32[]{:S(2)}, u32[]{:S(2)}) %collective-permute-start.12) | collective-permute-done | bytes 1048608 | tf_op jit(solution)/shard_map/ppermute | solution.py:48
  48.9 1.6 collective-permute-start.4
  50.5 1.7 shard_map.71
  52.2 21.1 %collective-permute-done.13.refs_2_ = f32[4,2,4,32,256]{4,3,2,1,0:T(8,128)S(1)} collective-permute-done((f32[4,2,4,32,256]{4,3,2,1,0:T(8,128)S(1)}, f32[4,2,4,32,256]{4,3,2,1,0:T(8,128)S(1)}, u32[]{:S(2)}, u32[]{:S(2)}) %collective-permute-start.13) | collective-permute-done | bytes 1048608 | tf_op jit(solution)/shard_map/ppermute | solution.py:48
  73.3 2.1 %collective-permute-done.14.refs_3_ = f32[4,2,4,32,256]{4,3,2,1,0:T(8,128)S(1)} collective-permute-done((f32[4,2,4,32,256]{4,3,2,1,0:T(8,128)S(1)}, f32[4,2,4,32,256]{4,3,2,1,0:T(8,128)S(1)}, u32[]{:S(2)}, u32[]{:S(2)}) %collective-permute-start.14) | collective-permute-done | bytes 1048608 | tf_op jit(solution)/shard_map/ppermute | solution.py:48
  75.4 0.7 shard_map.75
  76.1 2.2 %collective-permute-start.15 = (f32[2,4,4,32,256]{4,3,2,1,0:T(8,128)S(1)}, f32[2,4,4,32,256]{4,3,2,1,0:T(8,128)S(1)}, u32[]{:S(2)}, u32[]{:S(2)}) collective-permute-start(f32[2,4,4,32,256]{4,3,2,1,0:T(8,128)S(1)} %get-tuple-element.64), channel_id=1, source_target_pairs={{0,4},{4,0},{8,12},{12,8},{16,20},{20,16},{24,28},{28,24},{32,36},... | collective-permute-start | bytes 3145736 | tf_op jit(solution)/shard_map/ppermute | solution.py:48
  78.4 4.6 %collective-permute-done.3.refs_2_ = f32[4,4,2,32,256]{4,3,2,1,0:T(8,128)S(1)} collective-permute-done((f32[4,4,2,32,256]{4,3,2,1,0:T(8,128)S(1)}, f32[4,4,2,32,256]{4,3,2,1,0:T(8,128)S(1)}, u32[]{:S(2)}, u32[]{:S(2)}) %collective-permute-start.3) | collective-permute-done | bytes 1048608 | tf_op jit(solution)/shard_map/ppermute | solution.py:46
  83.0 12.7 %collective-permute-done.4.refs_3_ = f32[4,4,2,32,256]{4,3,2,1,0:T(8,128)S(1)} collective-permute-done((f32[4,4,2,32,256]{4,3,2,1,0:T(8,128)S(1)}, f32[4,4,2,32,256]{4,3,2,1,0:T(8,128)S(1)}, u32[]{:S(2)}, u32[]{:S(2)}) %collective-permute-start.4) | collective-permute-done | bytes 1048608 | tf_op jit(solution)/shard_map/ppermute | solution.py:46
  95.7 0.8 shard_map.72
  96.4 2.8 %collective-permute-start.5 = (f32[2,4,4,32,256]{4,3,2,1,0:T(8,128)S(1)}, f32[2,4,4,32,256]{4,3,2,1,0:T(8,128)S(1)}, u32[]{:S(2)}, u32[]{:S(2)}) collective-permute-start(f32[2,4,4,32,256]{4,3,2,1,0:T(8,128)S(1)} %get-tuple-element.49), channel_id=1, source_target_pairs={{0,4},{4,0},{8,12},{12,8},{16,20},{20,16},{24,28},{28,24},{32,36},... | collective-permute-start | bytes 3145736 | tf_op jit(solution)/shard_map/ppermute | solution.py:48
  99.7 2.6 %collective-permute-start.17 = (f32[2,4,32,256]{3,2,1,0:T(8,128)S(1)}, f32[2,4,32,256]{3,2,1,0:T(8,128)S(1)}, u32[]{:S(2)}, u32[]{:S(2)}) collective-permute-start(f32[2,4,32,256]{3,2,1,0:T(8,128)S(1)} %get-tuple-element.67), channel_id=1, source_target_pairs={{0,64},{4,68},{8,72},{12,76},{16,80},{20,84},{24,88},{28,92},{32,9... | collective-permute-start | bytes 786440 | tf_op jit(solution)/shard_map/ppermute | solution.py:48
  102.3 1.1 collective-permute-start.18
  103.6 2.8 %collective-permute-start.7 = (f32[2,4,32,256]{3,2,1,0:T(8,128)S(1)}, f32[2,4,32,256]{3,2,1,0:T(8,128)S(1)}, u32[]{:S(2)}, u32[]{:S(2)}) collective-permute-start(f32[2,4,32,256]{3,2,1,0:T(8,128)S(1)} %get-tuple-element.52), channel_id=1, source_target_pairs={{0,64},{4,68},{8,72},{12,76},{16,80},{20,84},{24,88},{28,92},{32,9... | collective-permute-start | bytes 786440 | tf_op jit(solution)/shard_map/ppermute | solution.py:48
  106.4 0.9 collective-permute-done.16.refs_1_
  107.3 1.6 collective-permute-start.8
  108.9 5.4 %collective-permute-done.17.refs_2_ = f32[2,4,32,256]{3,2,1,0:T(8,128)S(1)} collective-permute-done((f32[2,4,32,256]{3,2,1,0:T(8,128)S(1)}, f32[2,4,32,256]{3,2,1,0:T(8,128)S(1)}, u32[]{:S(2)}, u32[]{:S(2)}) %collective-permute-start.17) | collective-permute-done | bytes 262176 | tf_op jit(solution)/shard_map/ppermute | solution.py:48
  114.3 2.1 %collective-permute-done.18.refs_3_ = f32[2,4,32,256]{3,2,1,0:T(8,128)S(1)} collective-permute-done((f32[2,4,32,256]{3,2,1,0:T(8,128)S(1)}, f32[2,4,32,256]{3,2,1,0:T(8,128)S(1)}, u32[]{:S(2)}, u32[]{:S(2)}) %collective-permute-start.18) | collective-permute-done | bytes 262176 | tf_op jit(solution)/shard_map/ppermute | solution.py:48
  116.6 3.8 %collective-permute-start.20 = (f32[2,32,256]{2,1,0:T(8,128)S(1)}, f32[2,32,256]{2,1,0:T(8,128)S(1)}, u32[]{:S(2)}, u32[]{:S(2)}) collective-permute-start(f32[2,32,256]{2,1,0:T(8,128)S(1)} %get-tuple-element.71), channel_id=1, source_target_pairs={{0,2},{1,3},{2,0},{3,1},{4,6},{5,7},{6,4},{7,5},{8,10},{9,11},{10,... | collective-permute-start | bytes 196616 | tf_op jit(solution)/shard_map/ppermute | solution.py:46
  120.4 5.2 %collective-permute-done.7.refs_2_ = f32[2,4,32,256]{3,2,1,0:T(8,128)S(1)} collective-permute-done((f32[2,4,32,256]{3,2,1,0:T(8,128)S(1)}, f32[2,4,32,256]{3,2,1,0:T(8,128)S(1)}, u32[]{:S(2)}, u32[]{:S(2)}) %collective-permute-start.7) | collective-permute-done | bytes 262176 | tf_op jit(solution)/shard_map/ppermute | solution.py:48
  125.6 2.0 %collective-permute-done.8.refs_3_ = f32[2,4,32,256]{3,2,1,0:T(8,128)S(1)} collective-permute-done((f32[2,4,32,256]{3,2,1,0:T(8,128)S(1)}, f32[2,4,32,256]{3,2,1,0:T(8,128)S(1)}, u32[]{:S(2)}, u32[]{:S(2)}) %collective-permute-start.8) | collective-permute-done | bytes 262176 | tf_op jit(solution)/shard_map/ppermute | solution.py:48
  127.7 1.3 collective-permute-start.9
  129.0 4.2 %collective-permute-start.10 = (f32[2,32,256]{2,1,0:T(8,128)S(1)}, f32[2,32,256]{2,1,0:T(8,128)S(1)}, u32[]{:S(2)}, u32[]{:S(2)}) collective-permute-start(f32[2,32,256]{2,1,0:T(8,128)S(1)} %get-tuple-element.56), channel_id=1, source_target_pairs={{0,16},{4,20},{8,24},{12,28},{16,0},{20,4},{24,8},{28,12},{32,48},... | collective-permute-start | bytes 196616 | tf_op jit(solution)/shard_map/ppermute | solution.py:48
  133.2 2.3 %collective-permute-done.10.refs_2_ = f32[2,32,256]{2,1,0:T(8,128)S(1)} collective-permute-done((f32[2,32,256]{2,1,0:T(8,128)S(1)}, f32[2,32,256]{2,1,0:T(8,128)S(1)}, u32[]{:S(2)}, u32[]{:S(2)}) %collective-permute-start.10) | collective-permute-done | bytes 65568 | tf_op jit(solution)/shard_map/ppermute | solution.py:48
  135.5 2.3 %collective-permute-done.11.refs_3_ = f32[2,32,256]{2,1,0:T(8,128)S(1)} collective-permute-done((f32[2,32,256]{2,1,0:T(8,128)S(1)}, f32[2,32,256]{2,1,0:T(8,128)S(1)}, u32[]{:S(2)}, u32[]{:S(2)}) %collective-permute-start.11) | collective-permute-done | bytes 65568 | tf_op jit(solution)/shard_map/ppermute | solution.py:48
  137.8 1.7 shard_map.78
  139.6 2.6 %collective-permute-start.22 = (f32[4,64,384]{2,1,0:T(8,128)S(1)}, f32[4,64,384]{2,1,0:T(8,128)S(1)}, u32[]{:S(2)}, u32[]{:S(2)}) collective-permute-start(f32[4,64,384]{2,1,0:T(8,128)S(1)} %get-tuple-element.75), channel_id=1, source_target_pairs={{0,4},{4,0},{8,12},{12,8},{16,20},{20,16},{24,28},{28,24},{32,36},... | collective-permute-start | bytes 1179656 | tf_op jit(solution)/shard_map/ppermute | solution.py:48
  142.2 1.3 collective-permute-done.22
  143.6 0.8 collective-permute-start.25
  144.4 2.5 %collective-permute-start.23 = (f32[64,384]{1,0:T(8,128)S(1)}, f32[64,384]{1,0:T(8,128)S(1)}, u32[]{:S(2)}, u32[]{:S(2)}) collective-permute-start(f32[64,384]{1,0:T(8,128)S(1)} %get-tuple-element.80), channel_id=1, source_target_pairs={{0,1},{1,0},{2,3},{3,2},{4,5},{5,4},{6,7},{7,6},{8,9},{9,8},{10,11... | collective-permute-start | bytes 294920 | tf_op jit(solution)/shard_map/ppermute | solution.py:46
  146.9 3.2 %collective-permute-done.25 = f32[64,384]{1,0:T(8,128)S(1)} collective-permute-done((f32[64,384]{1,0:T(8,128)S(1)}, f32[64,384]{1,0:T(8,128)S(1)}, u32[]{:S(2)}, u32[]{:S(2)}) %collective-permute-start.25) | collective-permute-done | bytes 98336 | tf_op jit(solution)/shard_map/ppermute | solution.py:46
  150.1 1.2 collective-permute-done.23
  151.6 3.0 %collective-permute-start.26 = (f32[64,384]{1,0:T(8,128)S(1)}, f32[64,384]{1,0:T(8,128)S(1)}, u32[]{:S(2)}, u32[]{:S(2)}) collective-permute-start(f32[64,384]{1,0:T(8,128)S(1)} %fusion.1), channel_id=1, source_target_pairs={{0,8},{4,12},{8,0},{12,4},{16,24},{20,28},{24,16},{28,20},{32,40},... | collective-permute-start | bytes 294920 | tf_op jit(solution)/shard_map/ppermute | solution.py:48
  154.6 2.9 %collective-permute-done.28 = f32[64,384]{1,0:T(8,128)S(1)} collective-permute-done((f32[64,384]{1,0:T(8,128)S(1)}, f32[64,384]{1,0:T(8,128)S(1)}, u32[]{:S(2)}, u32[]{:S(2)}) %collective-permute-start.28) | collective-permute-done | bytes 98336 | tf_op jit(solution)/shard_map/ppermute | solution.py:48
  158.0 0.9 collective-permute-start.31
  158.9 0.5 collective-permute-start.30
  159.4 2.0 %collective-permute-start.29 = (f32[64,384]{1,0:T(8,128)S(1)}, f32[64,384]{1,0:T(8,128)S(1)}, u32[]{:S(2)}, u32[]{:S(2)}) collective-permute-start(f32[64,384]{1,0:T(8,128)S(1)} %add_add_fusion.1), channel_id=1, source_target_pairs={{0,32},{4,36},{8,40},{12,44},{16,48},{20,52},{24,56},{28,60},{32,0... | collective-permute-start | bytes 294920 | tf_op jit(solution)/shard_map/ppermute | solution.py:48
  161.4 1.4 collective-permute-done.31
  162.8 1.1 collective-permute-done.30
  163.9 0.5 collective-permute-done.29
  164.4 0.9 collective-permute-start.34
  165.4 1.4 collective-permute-start.33
  166.8 1.0 collective-permute-start.32
  167.8 1.4 collective-permute-done.34.s3
  169.2 1.1 collective-permute-done.33.s2
  170.3 0.5 collective-permute-done.32.s1
  170.9 5.8 %collective-permute-start.35 = (f32[4,64,384]{2,1,0:T(8,128)S(1)}, f32[4,64,384]{2,1,0:T(8,128)S(1)}, u32[]{:S(2)}, u32[]{:S(2)}) collective-permute-start(f32[4,64,384]{2,1,0:T(8,128)S(1)} %pad_maximum_fusion), channel_id=1, source_target_pairs={{0,4},{4,0},{8,12},{12,8},{16,20},{20,16},{24,28},{28,24},{32,36},... | collective-permute-start | bytes 1179656 | tf_op jit(solution)/shard_map/ppermute | solution.py:48
  176.6 0.7 reshape.47
  177.4 0.6 collective-permute-done.35.p_ref
  178.0 16.3 %shard_map.79 = f32[512,512]{1,0:T(8,128)} custom-call(s32[4]{0:T(128)S(1)} %pad_add_fusion.ids_ref, f32[64,384]{1,0:T(8,128)S(1)} %add_add_fusion.s0, f32[64,384]{1,0:T(8,128)S(1)} %collective-permute-done.32.s1, f32[64,384]{1,0:T(8,128)S(1)} %collective-permute-done.33.s2, f32[64,384]{1,0:T(8,128)S(1)} %collective-permute-done.34.s3, ...), custom_call_target="tpu_custom_call" | custom-call | tf_op jit(solution)/shard_map/pallas_call | solution.py:417
  (39 shorter events, 2.2 us)
Async XLA Ops:
  1.4 11.4 %collective-permute-start.1 = (f32[16,512]{1,0:T(8,128)S(1)}, f32[16,512]{1,0:T(8,128)S(1)}, u32[]{:S(2)}, u32[]{:S(2)}) collective-permute-start(f32[16,512]{1,0:T(8,128)S(1)} %get-tuple-element.76), channel_id=1, source_target_pairs={{1,0},{2,1},{3,2},{4,3},{5,4},{6,5},{7,6},{8,7},{9,8},{10,9},{11,1... | collective-permute-start | bytes 98312 | tf_op jit(solution)/shard_map/ppermute | solution.py:343
  8.5 6.4 %collective-permute-start = (f32[16,512]{1,0:T(8,128)S(1)}, f32[16,512]{1,0:T(8,128)S(1)}, u32[]{:S(2)}, u32[]{:S(2)}) collective-permute-start(f32[16,512]{1,0:T(8,128)S(1)} %get-tuple-element.77), channel_id=1, source_target_pairs={{0,1},{1,2},{2,3},{3,4},{4,5},{5,6},{6,7},{7,8},{8,9},{9,10},{10,1... | collective-permute-start | bytes 98312 | tf_op jit(solution)/shard_map/ppermute | solution.py:342
  10.5 0.7 copy-start.3
  11.2 0.7 copy-start.4
  14.9 3.4 %copy-start = (f32[4096,512]{1,0:T(8,128)S(1)}, f32[4096,512]{1,0:T(8,128)}, u32[]{:S(2)}) copy-start(f32[4096,512]{1,0:T(8,128)} %x_ref.3) | copy-start | bytes 25165828
  18.3 0.9 copy-start.1
  19.2 31.3 %copy-start.2 = (s32[8192]{0:T(1024)S(1)}, s32[8192]{0:T(1024)}, u32[]{:S(2)}) copy-start(s32[8192]{0:T(1024)} %param.8) | copy-start | bytes 98308
  24.2 24.7 %collective-permute-start.12 = (f32[4,2,4,32,256]{4,3,2,1,0:T(8,128)S(1)}, f32[4,2,4,32,256]{4,3,2,1,0:T(8,128)S(1)}, u32[]{:S(2)}, u32[]{:S(2)}) collective-permute-start(f32[4,2,4,32,256]{4,3,2,1,0:T(8,128)S(1)} %bitcast.43), channel_id=1, source_target_pairs={{0,8},{4,12},{8,0},{12,4},{16,24},{20,28},{24,16},{28,20},{32,40},... | collective-permute-start | bytes 3145736 | tf_op jit(solution)/shard_map/ppermute | solution.py:48
  25.9 47.4 %collective-permute-start.13 = (f32[4,2,4,32,256]{4,3,2,1,0:T(8,128)S(1)}, f32[4,2,4,32,256]{4,3,2,1,0:T(8,128)S(1)}, u32[]{:S(2)}, u32[]{:S(2)}) collective-permute-start(f32[4,2,4,32,256]{4,3,2,1,0:T(8,128)S(1)} %bitcast.42), channel_id=1, source_target_pairs={{0,16},{4,20},{8,24},{12,28},{16,0},{20,4},{24,8},{28,12},{32,48},... | collective-permute-start | bytes 3145736 | tf_op jit(solution)/shard_map/ppermute | solution.py:48
  28.3 47.1 %collective-permute-start.14 = (f32[4,2,4,32,256]{4,3,2,1,0:T(8,128)S(1)}, f32[4,2,4,32,256]{4,3,2,1,0:T(8,128)S(1)}, u32[]{:S(2)}, u32[]{:S(2)}) collective-permute-start(f32[4,2,4,32,256]{4,3,2,1,0:T(8,128)S(1)} %bitcast.41), channel_id=1, source_target_pairs={{0,24},{4,28},{8,16},{12,20},{16,8},{20,12},{24,0},{28,4},{32,56},... | collective-permute-start | bytes 3145736 | tf_op jit(solution)/shard_map/ppermute | solution.py:48
  33.6 44.8 %collective-permute-start.2 = (f32[4,4,2,32,256]{4,3,2,1,0:T(8,128)S(1)}, f32[4,4,2,32,256]{4,3,2,1,0:T(8,128)S(1)}, u32[]{:S(2)}, u32[]{:S(2)}) collective-permute-start(f32[4,4,2,32,256]{4,3,2,1,0:T(8,128)S(1)} %bitcast.40), channel_id=1, source_target_pairs={{0,1},{1,0},{2,3},{3,2},{4,5},{5,4},{6,7},{7,6},{8,9},{9,8},{10,11... | collective-permute-start | bytes 3145736 | tf_op jit(solution)/shard_map/ppermute | solution.py:46
  33.7 49.3 %collective-permute-start.3 = (f32[4,4,2,32,256]{4,3,2,1,0:T(8,128)S(1)}, f32[4,4,2,32,256]{4,3,2,1,0:T(8,128)S(1)}, u32[]{:S(2)}, u32[]{:S(2)}) collective-permute-start(f32[4,4,2,32,256]{4,3,2,1,0:T(8,128)S(1)} %bitcast.39), channel_id=1, source_target_pairs={{0,2},{1,3},{2,0},{3,1},{4,6},{5,7},{6,4},{7,5},{8,10},{9,11},{10,... | collective-permute-start | bytes 3145736 | tf_op jit(solution)/shard_map/ppermute | solution.py:46
  48.9 46.7 %collective-permute-start.4 = (f32[4,4,2,32,256]{4,3,2,1,0:T(8,128)S(1)}, f32[4,4,2,32,256]{4,3,2,1,0:T(8,128)S(1)}, u32[]{:S(2)}, u32[]{:S(2)}) collective-permute-start(f32[4,4,2,32,256]{4,3,2,1,0:T(8,128)S(1)} %bitcast.38), channel_id=1, source_target_pairs={{0,3},{1,2},{2,1},{3,0},{4,7},{5,6},{6,5},{7,4},{8,11},{9,10},{10,... | collective-permute-start | bytes 3145736 | tf_op jit(solution)/shard_map/ppermute | solution.py:46
  76.1 23.1 %collective-permute-start.15 = (f32[2,4,4,32,256]{4,3,2,1,0:T(8,128)S(1)}, f32[2,4,4,32,256]{4,3,2,1,0:T(8,128)S(1)}, u32[]{:S(2)}, u32[]{:S(2)}) collective-permute-start(f32[2,4,4,32,256]{4,3,2,1,0:T(8,128)S(1)} %get-tuple-element.64), channel_id=1, source_target_pairs={{0,4},{4,0},{8,12},{12,8},{16,20},{20,16},{24,28},{28,24},{32,36},... | collective-permute-start | bytes 3145736 | tf_op jit(solution)/shard_map/ppermute | solution.py:48
  96.4 6.9 %collective-permute-start.5 = (f32[2,4,4,32,256]{4,3,2,1,0:T(8,128)S(1)}, f32[2,4,4,32,256]{4,3,2,1,0:T(8,128)S(1)}, u32[]{:S(2)}, u32[]{:S(2)}) collective-permute-start(f32[2,4,4,32,256]{4,3,2,1,0:T(8,128)S(1)} %get-tuple-element.49), channel_id=1, source_target_pairs={{0,4},{4,0},{8,12},{12,8},{16,20},{20,16},{24,28},{28,24},{32,36},... | collective-permute-start | bytes 3145736 | tf_op jit(solution)/shard_map/ppermute | solution.py:48
  99.4 7.9 %collective-permute-start.16 = (f32[2,4,32,256]{3,2,1,0:T(8,128)S(1)}, f32[2,4,32,256]{3,2,1,0:T(8,128)S(1)}, u32[]{:S(2)}, u32[]{:S(2)}) collective-permute-start(f32[2,4,32,256]{3,2,1,0:T(8,128)S(1)} %get-tuple-element.66), channel_id=1, source_target_pairs={{0,32},{4,36},{8,40},{12,44},{16,48},{20,52},{24,56},{28,60},{32,0... | collective-permute-start | bytes 786440 | tf_op jit(solution)/shard_map/ppermute | solution.py:48
  99.7 14.6 %collective-permute-start.17 = (f32[2,4,32,256]{3,2,1,0:T(8,128)S(1)}, f32[2,4,32,256]{3,2,1,0:T(8,128)S(1)}, u32[]{:S(2)}, u32[]{:S(2)}) collective-permute-start(f32[2,4,32,256]{3,2,1,0:T(8,128)S(1)} %get-tuple-element.67), channel_id=1, source_target_pairs={{0,64},{4,68},{8,72},{12,76},{16,80},{20,84},{24,88},{28,92},{32,9... | collective-permute-start | bytes 786440 | tf_op jit(solution)/shard_map/ppermute | solution.py:48
  102.3 14.1 %collective-permute-start.18 = (f32[2,4,32,256]{3,2,1,0:T(8,128)S(1)}, f32[2,4,32,256]{3,2,1,0:T(8,128)S(1)}, u32[]{:S(2)}, u32[]{:S(2)}) collective-permute-start(f32[2,4,32,256]{3,2,1,0:T(8,128)S(1)} %get-tuple-element.68), channel_id=1, source_target_pairs={{0,96},{4,100},{8,104},{12,108},{16,112},{20,116},{24,120},{28,124... | collective-permute-start | bytes 786440 | tf_op jit(solution)/shard_map/ppermute | solution.py:48
  103.5 16.9 %collective-permute-start.6 = (f32[2,4,32,256]{3,2,1,0:T(8,128)S(1)}, f32[2,4,32,256]{3,2,1,0:T(8,128)S(1)}, u32[]{:S(2)}, u32[]{:S(2)}) collective-permute-start(f32[2,4,32,256]{3,2,1,0:T(8,128)S(1)} %get-tuple-element.51), channel_id=1, source_target_pairs={{0,32},{4,36},{8,40},{12,44},{16,48},{20,52},{24,56},{28,60},{32,0... | collective-permute-start | bytes 786440 | tf_op jit(solution)/shard_map/ppermute | solution.py:48
  103.6 22.0 %collective-permute-start.7 = (f32[2,4,32,256]{3,2,1,0:T(8,128)S(1)}, f32[2,4,32,256]{3,2,1,0:T(8,128)S(1)}, u32[]{:S(2)}, u32[]{:S(2)}) collective-permute-start(f32[2,4,32,256]{3,2,1,0:T(8,128)S(1)} %get-tuple-element.52), channel_id=1, source_target_pairs={{0,64},{4,68},{8,72},{12,76},{16,80},{20,84},{24,88},{28,92},{32,9... | collective-permute-start | bytes 786440 | tf_op jit(solution)/shard_map/ppermute | solution.py:48
  107.3 20.3 %collective-permute-start.8 = (f32[2,4,32,256]{3,2,1,0:T(8,128)S(1)}, f32[2,4,32,256]{3,2,1,0:T(8,128)S(1)}, u32[]{:S(2)}, u32[]{:S(2)}) collective-permute-start(f32[2,4,32,256]{3,2,1,0:T(8,128)S(1)} %get-tuple-element.53), channel_id=1, source_target_pairs={{0,96},{4,100},{8,104},{12,108},{16,112},{20,116},{24,120},{28,124... | collective-permute-start | bytes 786440 | tf_op jit(solution)/shard_map/ppermute | solution.py:48
  116.5 16.7 %collective-permute-start.19 = (f32[2,32,256]{2,1,0:T(8,128)S(1)}, f32[2,32,256]{2,1,0:T(8,128)S(1)}, u32[]{:S(2)}, u32[]{:S(2)}) collective-permute-start(f32[2,32,256]{2,1,0:T(8,128)S(1)} %get-tuple-element.70), channel_id=1, source_target_pairs={{0,1},{1,0},{2,3},{3,2},{4,5},{5,4},{6,7},{7,6},{8,9},{9,8},{10,11... | collective-permute-start | bytes 196616 | tf_op jit(solution)/shard_map/ppermute | solution.py:46
  116.6 16.6 %collective-permute-start.20 = (f32[2,32,256]{2,1,0:T(8,128)S(1)}, f32[2,32,256]{2,1,0:T(8,128)S(1)}, u32[]{:S(2)}, u32[]{:S(2)}) collective-permute-start(f32[2,32,256]{2,1,0:T(8,128)S(1)} %get-tuple-element.71), channel_id=1, source_target_pairs={{0,2},{1,3},{2,0},{3,1},{4,6},{5,7},{6,4},{7,5},{8,10},{9,11},{10,... | collective-permute-start | bytes 196616 | tf_op jit(solution)/shard_map/ppermute | solution.py:46
  120.4 12.8 %collective-permute-start.21 = (f32[2,32,256]{2,1,0:T(8,128)S(1)}, f32[2,32,256]{2,1,0:T(8,128)S(1)}, u32[]{:S(2)}, u32[]{:S(2)}) collective-permute-start(f32[2,32,256]{2,1,0:T(8,128)S(1)} %get-tuple-element.72), channel_id=1, source_target_pairs={{0,3},{1,2},{2,1},{3,0},{4,7},{5,6},{6,5},{7,4},{8,11},{9,10},{10,... | collective-permute-start | bytes 196616 | tf_op jit(solution)/shard_map/ppermute | solution.py:46
  127.7 5.5 %collective-permute-start.9 = (f32[2,32,256]{2,1,0:T(8,128)S(1)}, f32[2,32,256]{2,1,0:T(8,128)S(1)}, u32[]{:S(2)}, u32[]{:S(2)}) collective-permute-start(f32[2,32,256]{2,1,0:T(8,128)S(1)} %get-tuple-element.55), channel_id=1, source_target_pairs={{0,8},{4,12},{8,0},{12,4},{16,24},{20,28},{24,16},{28,20},{32,40},... | collective-permute-start | bytes 196616 | tf_op jit(solution)/shard_map/ppermute | solution.py:48
  129.0 6.5 %collective-permute-start.10 = (f32[2,32,256]{2,1,0:T(8,128)S(1)}, f32[2,32,256]{2,1,0:T(8,128)S(1)}, u32[]{:S(2)}, u32[]{:S(2)}) collective-permute-start(f32[2,32,256]{2,1,0:T(8,128)S(1)} %get-tuple-element.56), channel_id=1, source_target_pairs={{0,16},{4,20},{8,24},{12,28},{16,0},{20,4},{24,8},{28,12},{32,48},... | collective-permute-start | bytes 196616 | tf_op jit(solution)/shard_map/ppermute | solution.py:48
  133.2 4.7 %collective-permute-start.11 = (f32[2,32,256]{2,1,0:T(8,128)S(1)}, f32[2,32,256]{2,1,0:T(8,128)S(1)}, u32[]{:S(2)}, u32[]{:S(2)}) collective-permute-start(f32[2,32,256]{2,1,0:T(8,128)S(1)} %get-tuple-element.57), channel_id=1, source_target_pairs={{0,24},{4,28},{8,16},{12,20},{16,8},{20,12},{24,0},{28,4},{32,56},... | collective-permute-start | bytes 196616 | tf_op jit(solution)/shard_map/ppermute | solution.py:48
  139.6 4.0 %collective-permute-start.22 = (f32[4,64,384]{2,1,0:T(8,128)S(1)}, f32[4,64,384]{2,1,0:T(8,128)S(1)}, u32[]{:S(2)}, u32[]{:S(2)}) collective-permute-start(f32[4,64,384]{2,1,0:T(8,128)S(1)} %get-tuple-element.75), channel_id=1, source_target_pairs={{0,4},{4,0},{8,12},{12,8},{16,20},{20,16},{24,28},{28,24},{32,36},... | collective-permute-start | bytes 1179656 | tf_op jit(solution)/shard_map/ppermute | solution.py:48
  143.6 6.5 %collective-permute-start.25 = (f32[64,384]{1,0:T(8,128)S(1)}, f32[64,384]{1,0:T(8,128)S(1)}, u32[]{:S(2)}, u32[]{:S(2)}) collective-permute-start(f32[64,384]{1,0:T(8,128)S(1)} %get-tuple-element.78), channel_id=1, source_target_pairs={{0,3},{1,2},{2,1},{3,0},{4,7},{5,6},{6,5},{7,4},{8,11},{9,10},{10,... | collective-permute-start | bytes 294920 | tf_op jit(solution)/shard_map/ppermute | solution.py:46
  144.4 5.7 %collective-permute-start.24 = (f32[64,384]{1,0:T(8,128)S(1)}, f32[64,384]{1,0:T(8,128)S(1)}, u32[]{:S(2)}, u32[]{:S(2)}) collective-permute-start(f32[64,384]{1,0:T(8,128)S(1)} %get-tuple-element.79), channel_id=1, source_target_pairs={{0,2},{1,3},{2,0},{3,1},{4,6},{5,7},{6,4},{7,5},{8,10},{9,11},{10,... | collective-permute-start | bytes 294920 | tf_op jit(solution)/shard_map/ppermute | solution.py:46
  144.4 6.9 %collective-permute-start.23 = (f32[64,384]{1,0:T(8,128)S(1)}, f32[64,384]{1,0:T(8,128)S(1)}, u32[]{:S(2)}, u32[]{:S(2)}) collective-permute-start(f32[64,384]{1,0:T(8,128)S(1)} %get-tuple-element.80), channel_id=1, source_target_pairs={{0,1},{1,0},{2,3},{3,2},{4,5},{5,4},{6,7},{7,6},{8,9},{9,8},{10,11... | collective-permute-start | bytes 294920 | tf_op jit(solution)/shard_map/ppermute | solution.py:46
  151.3 6.2 %collective-permute-start.28 = (f32[64,384]{1,0:T(8,128)S(1)}, f32[64,384]{1,0:T(8,128)S(1)}, u32[]{:S(2)}, u32[]{:S(2)}) collective-permute-start(f32[64,384]{1,0:T(8,128)S(1)} %fusion.1), channel_id=1, source_target_pairs={{0,24},{4,28},{8,16},{12,20},{16,8},{20,12},{24,0},{28,4},{32,56},... | collective-permute-start | bytes 294920 | tf_op jit(solution)/shard_map/ppermute | solution.py:48
  151.4 6.1 %collective-permute-start.27 = (f32[64,384]{1,0:T(8,128)S(1)}, f32[64,384]{1,0:T(8,128)S(1)}, u32[]{:S(2)}, u32[]{:S(2)}) collective-permute-start(f32[64,384]{1,0:T(8,128)S(1)} %fusion.1), channel_id=1, source_target_pairs={{0,16},{4,20},{8,24},{12,28},{16,0},{20,4},{24,8},{28,12},{32,48},... | collective-permute-start | bytes 294920 | tf_op jit(solution)/shard_map/ppermute | solution.py:48
  151.6 6.4 %collective-permute-start.26 = (f32[64,384]{1,0:T(8,128)S(1)}, f32[64,384]{1,0:T(8,128)S(1)}, u32[]{:S(2)}, u32[]{:S(2)}) collective-permute-start(f32[64,384]{1,0:T(8,128)S(1)} %fusion.1), channel_id=1, source_target_pairs={{0,8},{4,12},{8,0},{12,4},{16,24},{20,28},{24,16},{28,20},{32,40},... | collective-permute-start | bytes 294920 | tf_op jit(solution)/shard_map/ppermute | solution.py:48
  158.0 4.8 %collective-permute-start.31 = (f32[64,384]{1,0:T(8,128)S(1)}, f32[64,384]{1,0:T(8,128)S(1)}, u32[]{:S(2)}, u32[]{:S(2)}) collective-permute-start(f32[64,384]{1,0:T(8,128)S(1)} %add_add_fusion.1), channel_id=1, source_target_pairs={{0,96},{4,100},{8,104},{12,108},{16,112},{20,116},{24,120},{28,124... | collective-permute-start | bytes 294920 | tf_op jit(solution)/shard_map/ppermute | solution.py:48
  158.9 5.0 %collective-permute-start.30 = (f32[64,384]{1,0:T(8,128)S(1)}, f32[64,384]{1,0:T(8,128)S(1)}, u32[]{:S(2)}, u32[]{:S(2)}) collective-permute-start(f32[64,384]{1,0:T(8,128)S(1)} %add_add_fusion.1), channel_id=1, source_target_pairs={{0,64},{4,68},{8,72},{12,76},{16,80},{20,84},{24,88},{28,92},{32,9... | collective-permute-start | bytes 294920 | tf_op jit(solution)/shard_map/ppermute | solution.py:48
  159.4 5.0 %collective-permute-start.29 = (f32[64,384]{1,0:T(8,128)S(1)}, f32[64,384]{1,0:T(8,128)S(1)}, u32[]{:S(2)}, u32[]{:S(2)}) collective-permute-start(f32[64,384]{1,0:T(8,128)S(1)} %add_add_fusion.1), channel_id=1, source_target_pairs={{0,32},{4,36},{8,40},{12,44},{16,48},{20,52},{24,56},{28,60},{32,0... | collective-permute-start | bytes 294920 | tf_op jit(solution)/shard_map/ppermute | solution.py:48
  164.4 4.8 %collective-permute-start.34 = (f32[64,384]{1,0:T(8,128)S(1)}, f32[64,384]{1,0:T(8,128)S(1)}, u32[]{:S(2)}, u32[]{:S(2)}) collective-permute-start(f32[64,384]{1,0:T(8,128)S(1)} %add_add_fusion.s0), channel_id=1, source_target_pairs={{0,3},{1,2},{2,1},{3,0},{4,7},{5,6},{6,5},{7,4},{8,11},{9,10},{10,... | collective-permute-start | bytes 294920 | tf_op jit(solution)/shard_map/ppermute | solution.py:46
  165.4 5.0 %collective-permute-start.33 = (f32[64,384]{1,0:T(8,128)S(1)}, f32[64,384]{1,0:T(8,128)S(1)}, u32[]{:S(2)}, u32[]{:S(2)}) collective-permute-start(f32[64,384]{1,0:T(8,128)S(1)} %add_add_fusion.s0), channel_id=1, source_target_pairs={{0,2},{1,3},{2,0},{3,1},{4,6},{5,7},{6,4},{7,5},{8,10},{9,11},{10,... | collective-permute-start | bytes 294920 | tf_op jit(solution)/shard_map/ppermute | solution.py:46
  166.8 4.1 %collective-permute-start.32 = (f32[64,384]{1,0:T(8,128)S(1)}, f32[64,384]{1,0:T(8,128)S(1)}, u32[]{:S(2)}, u32[]{:S(2)}) collective-permute-start(f32[64,384]{1,0:T(8,128)S(1)} %add_add_fusion.s0), channel_id=1, source_target_pairs={{0,1},{1,0},{2,3},{3,2},{4,5},{5,4},{6,7},{7,6},{8,9},{9,8},{10,11... | collective-permute-start | bytes 294920 | tf_op jit(solution)/shard_map/ppermute | solution.py:46
  170.9 7.1 %collective-permute-start.35 = (f32[4,64,384]{2,1,0:T(8,128)S(1)}, f32[4,64,384]{2,1,0:T(8,128)S(1)}, u32[]{:S(2)}, u32[]{:S(2)}) collective-permute-start(f32[4,64,384]{2,1,0:T(8,128)S(1)} %pad_maximum_fusion), channel_id=1, source_target_pairs={{0,4},{4,0},{8,12},{12,8},{16,20},{20,16},{24,28},{28,24},{32,36},... | collective-permute-start | bytes 1179656 | tf_op jit(solution)/shard_map/ppermute | solution.py:48
